TPU v7x, 16 devices: a 4x2x1 block of a 4x4x8 slice. The times are simulated.
16 devices in a mesh: dp: 2 (over y, z), sp: 8 (over x, core).
Axes of the slice: x: 4, y: 2, z: 1, core: 2. Of those that a mesh axis runs over, the one named last changes fastest.
The devices are a block of a 4x4x8 slice.
Arguments:
- tokens: bfloat16 [128, 4096], P('dp'), parts along dimension 0
- positions: int32 [128], P('dp'), parts along dimension 0
- k_cache: bfloat16 [128, 512, 8, 128], P('dp', 'sp'), parts along dimension 0
- v_cache: bfloat16 [128, 512, 8, 128], P('dp', 'sp'), parts along dimension 0
- w_q: bfloat16 [4096, 4096], replicated
- w_k: bfloat16 [4096, 1024], replicated
- w_v: bfloat16 [4096, 1024], replicated
- w_o: bfloat16 [4096, 4096], replicated
- attn_norm: bfloat16 [4096], replicated
- q_norm: bfloat16 [128], replicated
- k_norm: bfloat16 [128], replicated
Outputs:
- output 1: bfloat16 [128, 4096], P('dp'), parts along dimension 0
- output 2: bfloat16 [128, 512, 8, 128], P('dp', 'sp'), parts along dimension 0
- output 3: bfloat16 [128, 512, 8, 128], P('dp', 'sp'), parts along dimension 0
- output 4: bfloat16 [128, 2, 8, 128], P('dp'), parts along dimension 0
There are 2 independent parts. A program takes and returns all parts, laid end to end along the dimension named above; an argument that names none is the same for every part.
All inputs are finite; a program needn't handle non-finite values.
Results may differ from a plain program's by a relative error of at most 0.00658311.
Values sent between devices are 32-bit elements.
A program may use at most 768 MiB of HBM per device.

v0:
```python
import jax
import jax.numpy as jnp
from jax import lax
from jax.sharding import PartitionSpec as P

NORM_EPS = 1e-6
ROPE_THETA = 1000000.0
NEG_FILL = -1e30


def rms_scale(values, gain):
    return values * lax.rsqrt(jnp.mean(values * values, axis=-1, keepdims=True) + NORM_EPS) * gain.astype(jnp.float32)


def rope_table(positions, head_dim):
    inv_freq = ROPE_THETA ** (-jnp.arange(head_dim // 2, dtype=jnp.float32) * 2.0 / head_dim)
    angles = positions.astype(jnp.float32)[:, None] * inv_freq[None, :]
    return jnp.cos(angles)[:, None, :], jnp.sin(angles)[:, None, :]


def norm_rope(proj, gain, cos_table, sin_table):
    normed = rms_scale(proj.astype(jnp.float32), gain)
    half_dim = proj.shape[-1] // 2
    first_half = normed[..., :half_dim]
    second_half = normed[..., half_dim:]
    rotated = jnp.concatenate([first_half * cos_table - second_half * sin_table, second_half * cos_table + first_half * sin_table], axis=-1)
    return rotated.astype(jnp.bfloat16)


def project_token(tokens, positions, w_q, w_k, w_v, attn_norm, q_norm, k_norm):
    seq_count = tokens.shape[0]
    head_dim = q_norm.shape[0]
    hidden = rms_scale(tokens.astype(jnp.float32), attn_norm).astype(jnp.bfloat16)
    q_proj = jnp.dot(hidden, w_q, preferred_element_type=jnp.float32).astype(jnp.bfloat16).reshape(seq_count, -1, head_dim)
    k_proj = jnp.dot(hidden, w_k, preferred_element_type=jnp.float32).astype(jnp.bfloat16).reshape(seq_count, -1, head_dim)
    v_new = jnp.dot(hidden, w_v, preferred_element_type=jnp.float32).astype(jnp.bfloat16).reshape(seq_count, -1, head_dim)
    cos_table, sin_table = rope_table(positions, head_dim)
    return norm_rope(q_proj, q_norm, cos_table, sin_table), norm_rope(k_proj, k_norm, cos_table, sin_table), v_new


def local_attention(q_rot, k_rot, v_new, positions, k_loc, v_loc, shard_start):
    seq_count, slot_count, kv_heads, head_dim = k_loc.shape
    q_per_kv = q_rot.shape[1] // kv_heads
    score_scale = head_dim ** -0.5
    slot_ids = shard_start + jnp.arange(slot_count)
    write_mask = (slot_ids[None, :] == positions[:, None])[:, :, None, None]
    k_upd = jnp.where(write_mask, k_rot[:, None], k_loc)
    v_upd = jnp.where(write_mask, v_new[:, None], v_loc)
    q_grp = q_rot.reshape(seq_count, kv_heads, q_per_kv, head_dim)
    scores = jnp.einsum('bkgd,btkd->bkgt', q_grp, k_upd, preferred_element_type=jnp.float32) * score_scale
    live_mask = (slot_ids[None, :] <= positions[:, None])[:, None, None, :]
    local_peak = jnp.max(jnp.where(live_mask, scores, NEG_FILL), axis=-1)
    weights = jnp.where(live_mask, jnp.exp(scores - local_peak[..., None]), 0.0)
    local_sum = jnp.sum(weights, axis=-1)
    local_out = jnp.einsum('bkgt,btkd->bkgd', weights.astype(jnp.bfloat16), v_upd, preferred_element_type=jnp.float32)
    return k_upd, v_upd, local_peak, local_sum, local_out


def solution(mesh):
    cache_spec = P('dp', 'sp', None, None)

    def device_step(tokens, positions, k_cache, v_cache, w_q, w_k, w_v, w_o, attn_norm, q_norm, k_norm):
        q_rot, k_rot, v_new = project_token(tokens, positions, w_q, w_k, w_v, attn_norm, q_norm, k_norm)
        head_dim = q_norm.shape[0]
        shard_start = lax.axis_index('sp') * k_cache.shape[1]
        k_upd, v_upd, local_peak, local_sum, local_out = local_attention(q_rot, k_rot, v_new, positions, k_cache, v_cache, shard_start)
        global_peak = lax.pmax(local_peak, 'sp')
        factor = jnp.exp(local_peak - global_peak)
        packed = jnp.concatenate([local_out * factor[..., None], (local_sum * factor)[..., None]], axis=-1)
        summed = lax.psum(packed, 'sp')
        attn_out = (summed[..., :head_dim] / summed[..., head_dim:]).astype(jnp.bfloat16).reshape(tokens.shape[0], -1)
        block_out = (tokens.astype(jnp.float32) + jnp.dot(attn_out, w_o, preferred_element_type=jnp.float32)).astype(jnp.bfloat16)
        return block_out, k_upd, v_upd, jnp.stack([k_rot, v_new], axis=1)

    return jax.shard_map(device_step, mesh=mesh, in_specs=(P('dp', None), P('dp'), cache_spec, cache_spec, P(), P(), P(), P(), P(), P(), P()), out_specs=(P('dp', None), cache_spec, cache_spec, P('dp', None, None, None)), check_vma=False)
```

profile of v0, /device:TPU:113, one launch (start us, length us, event | category | flops | bytes accessed | tf_op | source)
XLA Modules:
  0.0 178.8 jit_solution(5479020098665475409)
XLA Ops:
  7.3 0.7 convert_element_type.66
  7.9 0.7 convert_element_type.71
  8.6 0.7 convert_element_type.67
  9.3 1.4 fusion.16
  10.7 0.7 broadcast_compare_fusion.1
  11.4 0.7 convert_element_type.61
  12.1 5.3 %fusion.15 = bf16[8,8,8,128]{3,1,2,0:T(8,128)(2,1)S(1)} fusion(bf16[4096,1024]{1,0:T(8,128)(2,1)} %param.17, bf16[64,4096]{1,0:T(8,128)(2,1)} %param.11, f32[4096]{0:T(1024)S(1)} %convert_element_type.61, f32[64]{0:T(128)S(1)} %add_rsqrt_fusion.2), kind=kOutput, calls=%fused_computation.20 | convolution fusion | flops 537985024 | bytes 9060608 | tf_op jit(solution)/shard_map/dot_general | solution.py:36
  17.5 1.6 fusion.14
  19.5 13.7 %fusion.6 = f32[8,8,32,128]{3,1,2,0:T(8,128)S(1)} fusion(bf16[4096,4096]{1,0:T(8,128)(2,1)} %param.15, bf16[64,4096]{1,0:T(8,128)(2,1)S(1)} %copy-done, f32[4096]{0:T(1024)S(1)} %convert_element_type.61, f32[64]{0:T(128)S(1)} %add_rsqrt_fusion.2), kind=kOutput, calls=%fused_computation.13 | convolution fusion | flops 2149056512 | bytes 35143936 | tf_op jit(solution)/shard_map/dot_general | solution.py:34
  35.3 9.5 %broadcast_select_fusion = (bf16[64,64,8,128]{3,2,1,0:T(8,128)(2,1)}, bf16[64,64,8,128]{3,2,1,0:T(8,128)(2,1)S(1)}) fusion(bf16[64,64,8,128]{3,2,1,0:T(8,128)(2,1)} %param.14, pred[64,64]{1,0:T(8,128)(4,1)S(1)} %get-tuple-element.13, bf16[64,8,128]{2,1,0:T(8,128)(2,1)S(1)} %bitcast.36, bf16[64,64,8,128]{3,2,1,0:T(8,128)(2,1)} %param.13, ...), kind=kLoop, calls=%fused_computation.4 | loop fusion | flops 8388608 | bytes 33820672 | tf_op jit(solution)/shard_map/jit(_where)/select_n | solution.py:48
  44.7 3.4 %copy-done.1 = bf16[64,64,8,128]{3,2,1,0:T(8,128)(2,1)} copy-done((bf16[64,64,8,128]{3,2,1,0:T(8,128)(2,1)}, bf16[64,64,8,128]{3,2,1,0:T(8,128)(2,1)S(1)}, u32[]{:S(2)}) %copy-start.1) | copy-done | bytes 8388632
  48.1 4.7 %select_reduce_fusion = (f32[64,8,4]{2,1,0:T(8,128)S(1)}, f32[64,8,4,64]{3,2,1,0:T(4,128)S(1)}) fusion(pred[64,64]{1,0:T(8,128)(4,1)S(1)} %get-tuple-element.12, bf16[64,64,8,128]{3,2,1,0:T(8,128)(2,1)S(1)} %get-tuple-element.11, bf16[64,8,4,64]{3,2,1,0:T(4,128)(2,1)S(1)} %bitcast.42, bf16[64,8,4,64]{3,2,1,0:T(4,128)(2,1)S(1)} %bitcast.41), kind=kOutput, calls=%fused_computation.26 | convolution fusion | flops 34994176 | bytes 9449472 | tf_op jit(solution)/shard_map/bkgd,btkd->bkgt/dot_general | solution.py:50
  52.9 26.9 %pmax.7 = f32[64,8,4]{2,1,0:T(8,128)S(1)} all-reduce(f32[64,8,4]{2,1,0:T(8,128)S(1)} %get-tuple-element.16), channel_id=1, replica_groups=mesh['dp'=2,'sp'=8] {'sp'}, use_global_device_ids=true, to_apply=%region_4.5 | all-reduce | flops 2048 | bytes 16384 | tf_op jit(solution)/shard_map/pmax | solution.py:67
  79.8 1.3 fusion.20
  81.1 0.8 multiply_bitcast_fusion
  81.9 3.2 %copy.50 = f32[64,8,4,1]{3,2,1,0:T(4,128)S(1)} copy(f32[64,8,4,1]{2,1,0,3:T(8,128)S(1)} %get-tuple-element.4) | data formatting | bytes 16384 | tf_op jit(solution)/shard_map/broadcast_in_dim | solution.py:69
  85.1 5.9 %fusion.10 = f32[64,8,4,128]{3,2,1,0:T(4,128)S(1)} fusion(bf16[64,64,8,128]{3,2,1,0:T(8,128)(2,1)} %get-tuple-element.10, f32[64,8,4,64]{3,2,1,0:T(4,128)S(1)} %get-tuple-element.17, f32[64,8,4]{2,1,0:T(8,128)} %get-tuple-element.5, f32[64,8,4]{2,1,0:T(8,128)S(1)} %get-tuple-element.16, pred[64,64]{1,0:T(8,128)(4,1)S(1)} %get-tuple-element.12), kind=kOutput, calls=%fused_computation.15 | convolution fusion | flops 34209792 | bytes 9981952 | tf_op jit(solution)/shard_map/bkgt,btkd->bkgd/dot_general | solution.py:55
  91.0 1.9 %pad_maximum_fusion = f32[64,8,4,129]{3,2,1,0:T(4,128)} fusion(f32[64,8,4,1]{3,2,1,0:T(4,128)S(1)} %copy.50, f32[64,8,4,128]{3,2,1,0:T(4,128)S(1)} %fusion.10), kind=kLoop, calls=%fused_computation.10 | loop fusion | flops 264192 | bytes 2113536 | tf_op jit(solution)/shard_map/concatenate | solution.py:69
  92.9 0.8 pad_maximum_fusion.1
  93.8 57.2 %all-reduce.2.cloned.1.call-done = f32[64,8,4,129]{3,2,1,0:T(4,128)} async-done(((f32[64,8,4,129]{3,2,1,0:T(4,128)}), f32[64,8,4,129]{3,2,1,0:T(4,128)}) %all-reduce.2.cloned.1.call-update) | async-done | bytes 1056784 | tf_op jit(solution)/shard_map/psum | solution.py:70
  150.9 1.3 slice.29
  152.2 3.1 %copy.57 = f32[64,8,4,1]{2,1,0,3:T(8,128)S(1)} copy(f32[64,8,4,1]{3,2,1,0:T(4,128)S(1)} %slice.29) | data formatting | bytes 16384 | tf_op jit(solution)/shard_map/div | solution.py:71
  155.3 1.8 fusion.19
  157.5 14.4 %fusion.4 = bf16[64,4096]{1,0:T(8,128)(2,1)} fusion(bf16[64,4096]{1,0:T(8,128)(2,1)S(1)} %reshape.191, bf16[4096,4096]{1,0:T(8,128)(2,1)} %param.18, bf16[64,4096]{1,0:T(8,128)(2,1)S(1)} %copy-done), kind=kOutput, calls=%fused_computation.7 | convolution fusion | flops 2148270080 | bytes 35127296 | tf_op jit(solution)/shard_map/dot_general | solution.py:72
  (29 shorter events, 2.9 us)
Async XLA Ops:
  7.2 143.8 %all-reduce.2.cloned.1.call-start = ((), (), s32[]{:S(2)}) async-start(), calls=%async_computation | async-start | bytes 4194304 | tf_op jit(solution)/shard_map/psum | solution.py:70
  9.3 8.2 %slice-start = ((s8[8388608]{0:T(1024)(128)(4,1)}), s8[4194304]{0:T(1024)(128)(4,1)S(1)}, s32[]{:S(2)}) async-start(s8[8388608]{0:T(1024)(128)(4,1)} %bitcast.32), calls=%async_computation.1 | async-start | bytes 8388608
  12.1 5.4 %slice-start.1 = ((s8[8388608]{0:T(1024)(128)(4,1)}), s8[4194304]{0:T(1024)(128)(4,1)S(1)}, s32[]{:S(2)}) async-start(s8[8388608]{0:T(1024)(128)(4,1)} %bitcast.32), calls=%async_computation.2 | async-start | bytes 8388608
  12.1 5.4 %copy-start = (bf16[64,4096]{1,0:T(8,128)(2,1)S(1)}, bf16[64,4096]{1,0:T(8,128)(2,1)}, u32[]{:S(2)}) copy-start(bf16[64,4096]{1,0:T(8,128)(2,1)} %param.11) | copy-start | bytes 1572868
  44.7 3.4 %copy-start.1 = (bf16[64,64,8,128]{3,2,1,0:T(8,128)(2,1)}, bf16[64,64,8,128]{3,2,1,0:T(8,128)(2,1)S(1)}, u32[]{:S(2)}) copy-start(bf16[64,64,8,128]{3,2,1,0:T(8,128)(2,1)S(1)} %get-tuple-element.11) | copy-start | bytes 25165828
Sparse Core Ops, SparseCore 0:
  93.1 57.8 all-reduce.1
where the time goes:
time: 181 us; the launch traced here: 179 us
  waiting for transfers between devices  57.2 us (32%)
  matrix products  45.7 us (25%)
  blocking collectives  26.9 us (15%)
  other arithmetic  22.8 us (13%)
  between operations  14.3 us (8%)
  local copies, waits for them, and re-layouts  11.8 us (7%)
    psum x1, waiting for transfers between devices, device_step(): summed = lax.psum(packed, 'sp')  57.2 us
    pmax x1, blocking collectives, device_step(): global_peak = lax.pmax(local_peak, 'sp')  26.9 us
    dot_general x1, matrix products, device_step(): jnp.dot(attn_out, w_o, preferred_element_type=jnp.float32)  14.4 us
    dot_general x1, matrix products, project_token(): jnp.dot(hidden, w_q, preferred_element_type=jnp.float32)  13.7 us
    select_n x1, other arithmetic, local_attention(): v_upd = jnp.where(write_mask, v_new[:, None], v_loc)  9.47 us
    dot_general x1, matrix products, local_attention(): jnp.einsum('bkgt,btkd->bkgd', weights.astype(jnp.bfloat16), v_upd, prefer...  5.92 us
    dot_general x1, matrix products, project_token(): jnp.dot(hidden, w_v, preferred_element_type=jnp.float32)  5.31 us
    dot_general x1, matrix products, local_attention(): jnp.einsum('bkgd,btkd->bkgt', q_grp, k_upd, preferred_element_type=jnp.fl...  4.73 us
  transfers between devices with their start and end apart: 1, of which 1 were waited for; matrix products, arithmetic and copies ran while one was open for 0% of the time, Pallas kernels for 0%

commit v1 on v0

v1 whole, which is shorter than its diff:
```python
import functools

import jax
import jax.numpy as jnp
from jax import lax
from jax.experimental import pallas as pl
from jax.experimental.pallas import tpu as pltpu
from jax.sharding import PartitionSpec as P

NORM_EPS = 1e-6
ROPE_THETA = 1000000.0
NEG_FILL = -1e30
MESH = pl.DeviceIdType.MESH
W_COLS = 512
W_SLOTS = 5
STAT_ROWS = 8


def rope_table(positions, head_dim):
    inv_freq = ROPE_THETA ** (-jnp.arange(head_dim // 2, dtype=jnp.float32) * 2.0 / head_dim)
    angles = positions.astype(jnp.float32)[:, None] * inv_freq[None, :]
    cos, sin = jnp.cos(angles), jnp.sin(angles)
    return jnp.concatenate([cos, cos], axis=-1), jnp.concatenate([-sin, sin], axis=-1)


def norm_rope(proj, gain, cos_full, sin_full):
    values = proj.astype(jnp.bfloat16).astype(jnp.float32)
    scale = lax.rsqrt(jnp.mean(values * values, axis=-1, keepdims=True) + NORM_EPS)
    normed = values * scale * gain
    turned = pltpu.roll(normed, normed.shape[-1] // 2, 1)
    return (normed * cos_full + turned * sin_full).astype(jnp.bfloat16).astype(jnp.float32)


def local_kernel(pos_ref, tok_ref, cos_ref, sin_ref, an_ref, qn_ref, kn_ref, wq_ref, wk_ref, wv_ref, kc_ref, vc_ref,
                 ko_ref, vo_ref, new_ref, part_ref,
                 hid, wbuf, kbuf, vbuf, qf, kf, vf, mstat, lstat, wsem, ksem, vsem, kosem, vosem):
    seqs, model = tok_ref.shape
    head_dim = qn_ref.shape[-1]
    slots, kv_heads = kbuf.shape[1], kbuf.shape[2]
    groups = ksem.shape[0]
    per_group = seqs // groups
    q_heads = wq_ref.shape[1] // head_dim
    start = lax.axis_index('sp') * slots
    n_k = wk_ref.shape[1] // W_COLS
    n_q = wq_ref.shape[1] // W_COLS
    n_all = 2 * n_k + n_q
    heads_per = W_COLS // head_dim

    def w_copy(ref, col, n):
        slot = n % W_SLOTS if isinstance(n, int) else lax.rem(n, W_SLOTS)
        off = col * W_COLS if isinstance(col, int) else pl.multiple_of(col * W_COLS, W_COLS)
        return pltpu.make_async_copy(ref.at[:, pl.ds(off, W_COLS)], wbuf.at[slot], wsem.at[slot])

    def w_start(n):
        if n < n_k:
            w_copy(wk_ref, n, n).start()
        elif n < 2 * n_k:
            w_copy(wv_ref, n - n_k, n).start()
        else:
            w_copy(wq_ref, n - 2 * n_k, n).start()

    def cache_in(ref, buf, sem, g):
        rows = pl.ds(g * per_group, per_group)
        return pltpu.make_async_copy(ref.at[rows], buf.at[rows], sem.at[g])

    for n in range(W_SLOTS):
        w_start(n)

    blk = 512
    total = jnp.zeros((seqs, 1), jnp.float32)
    for i in range(model // blk):
        xf = tok_ref[:, i * blk:(i + 1) * blk].astype(jnp.float32)
        total = total + jnp.sum(xf * xf, axis=-1, keepdims=True)
    inv = lax.rsqrt(total / model + NORM_EPS)
    for i in range(model // blk):
        xf = tok_ref[:, i * blk:(i + 1) * blk].astype(jnp.float32)
        gain = an_ref[:, i * blk:(i + 1) * blk].astype(jnp.float32)
        hid[:, i * blk:(i + 1) * blk] = (xf * inv * gain).astype(jnp.bfloat16)

    cos_full, sin_full = cos_ref[...], sin_ref[...]

    def project(n):
        slot = n % W_SLOTS if isinstance(n, int) else lax.rem(n, W_SLOTS)
        w_copy(wq_ref, 0, n).wait()
        return jnp.dot(hid[...], wbuf[slot], preferred_element_type=jnp.float32)

    k_gain = kn_ref[...].astype(jnp.float32)
    q_gain = qn_ref[...].astype(jnp.float32)
    for n in range(2 * n_k):
        y = project(n)
        if n + W_SLOTS < n_all:
            w_start(n + W_SLOTS)
        for hh in range(heads_per):
            piece = y[:, hh * head_dim:(hh + 1) * head_dim]
            if n < n_k:
                row = (n * heads_per + hh) * seqs
                kf[row:row + seqs, :] = norm_rope(piece, k_gain, cos_full, sin_full)
            else:
                row = ((n - n_k) * heads_per + hh) * seqs
                vf[row:row + seqs, :] = piece.astype(jnp.bfloat16).astype(jnp.float32)

    def q_step(i, carry):
        n = i + 2 * n_k
        y = project(n)

        @pl.when(n + W_SLOTS < n_all)
        def _():
            w_copy(wq_ref, i + W_SLOTS, n + W_SLOTS).start()

        @pl.when(n + W_SLOTS >= n_all)
        def _():
            g = n + W_SLOTS - n_all
            cache_in(kc_ref, kbuf, ksem, g).start()
            cache_in(vc_ref, vbuf, vsem, g).start()

        for hh in range(heads_per):
            row = pl.multiple_of(i * (heads_per * seqs) + hh * seqs, seqs)
            qf[pl.ds(row, seqs), :] = norm_rope(y[:, hh * head_dim:(hh + 1) * head_dim], q_gain, cos_full, sin_full)
        return carry

    lax.fori_loop(0, n_q, q_step, 0)
    for g in range(W_SLOTS, groups):
        cache_in(kc_ref, kbuf, ksem, g).start()
        cache_in(vc_ref, vbuf, vsem, g).start()

    half = q_heads // 2
    cols = slots * kv_heads
    row_id = lax.broadcasted_iota(jnp.int32, (q_heads, cols), 0)
    col_id = lax.broadcasted_iota(jnp.int32, (q_heads, cols), 1)
    q_per_kv = q_heads // kv_heads
    head_ok = ((row_id % half) * 2) // q_per_kv == col_id % kv_heads
    slot_key = jnp.where(head_ok, col_id // kv_heads, slots * 1024)
    lane = lax.broadcasted_iota(jnp.int32, (q_heads, 128), 1)
    score_scale = head_dim ** -0.5
    part_rows = part_ref.shape[1]
    mstat[...] = jnp.zeros_like(mstat)
    lstat[...] = jnp.zeros_like(lstat)

    def group_step(g, carry):
        cache_in(kc_ref, kbuf, ksem, g).wait()
        cache_in(vc_ref, vbuf, vsem, g).wait()
        m_acc, l_acc = mstat[...], lstat[...]
        for bb in range(per_group):
            b = g * per_group + bb
            local = pos_ref[b] - start
            k_new = kf[pl.ds(b, kv_heads, stride=seqs), :].astype(jnp.bfloat16)
            v_new = vf[pl.ds(b, kv_heads, stride=seqs), :].astype(jnp.bfloat16)
            new_ref[b, 0] = k_new
            new_ref[b, 1] = v_new

            @pl.when((local >= 0) & (local < slots))
            def _():
                kbuf[b, local] = k_new
                vbuf[b, local] = v_new

            q_even = qf[pl.ds(b, half, stride=2 * seqs), :]
            q_odd = qf[pl.ds(b + seqs, half, stride=2 * seqs), :]
            q_b = jnp.concatenate([q_even, q_odd], axis=0).astype(jnp.bfloat16)
            k_b = kbuf[b].reshape(cols, head_dim)
            v_b = vbuf[b].reshape(cols, head_dim)
            s = lax.dot_general(q_b, k_b, (((1,), (1,)), ((), ())), preferred_element_type=jnp.float32) * score_scale
            live = slot_key <= local
            s = jnp.where(live, s, NEG_FILL)
            m = jnp.max(s, axis=-1, keepdims=True)
            e = jnp.where(live, jnp.exp(s - m), 0.0)
            l = jnp.sum(e, axis=-1, keepdims=True)
            o = jnp.dot(e.astype(jnp.bfloat16), v_b, preferred_element_type=jnp.float32)
            for par in range(2):
                for i in range(half):
                    part_ref[i, pl.ds(b + par * seqs, 1), :] = o[par * half + i:par * half + i + 1, :]
            m_acc = jnp.where(lane == b, m, m_acc)
            l_acc = jnp.where(lane == b, l, l_acc)
        mstat[...] = m_acc
        lstat[...] = l_acc
        rows = pl.ds(g * per_group, per_group)
        pltpu.make_async_copy(kbuf.at[rows], ko_ref.at[rows], kosem.at[g]).start()
        pltpu.make_async_copy(vbuf.at[rows], vo_ref.at[rows], vosem.at[g]).start()
        return carry

    lax.fori_loop(0, groups, group_step, 0)

    for i in range(half):
        base = 2 * seqs
        part_ref[i, base:base + 1, :] = mstat[i:i + 1, :]
        part_ref[i, base + 1:base + 2, :] = mstat[half + i:half + i + 1, :]
        part_ref[i, base + 2:base + 3, :] = lstat[i:i + 1, :]
        part_ref[i, base + 3:base + 4, :] = lstat[half + i:half + i + 1, :]
        part_ref[i, base + 4:base + 8, :] = jnp.zeros((4, 128), jnp.float32)
    for g in range(groups):
        rows = pl.ds(g * per_group, per_group)
        pltpu.make_async_copy(kbuf.at[rows], ko_ref.at[rows], kosem.at[g]).wait()
        pltpu.make_async_copy(vbuf.at[rows], vo_ref.at[rows], vosem.at[g]).wait()


def local_stage(tokens, positions, cos_t, sin_t, k_cache, v_cache, w_q, w_k, w_v, attn_norm, q_norm, k_norm):
    seqs, model = tokens.shape
    slots, kv_heads, head_dim = k_cache.shape[1:]
    q_heads = w_q.shape[1] // head_dim
    groups = 8
    vmem = pl.BlockSpec(memory_space=pltpu.VMEM)
    anyspec = pl.BlockSpec(memory_space=pl.ANY)
    part_shape = (q_heads // 2, 2 * seqs + STAT_ROWS, head_dim)
    return pl.pallas_call(
        local_kernel,
        name='local_stage',
        out_shape=(
            jax.ShapeDtypeStruct(k_cache.shape, k_cache.dtype),
            jax.ShapeDtypeStruct(v_cache.shape, v_cache.dtype),
            jax.ShapeDtypeStruct((seqs, 2, kv_heads, head_dim), jnp.bfloat16),
            jax.ShapeDtypeStruct(part_shape, jnp.float32),
        ),
        in_specs=[pl.BlockSpec(memory_space=pltpu.SMEM)] + [vmem] * 6 + [anyspec] * 5,
        out_specs=(anyspec, anyspec, vmem, vmem),
        scratch_shapes=[
            pltpu.VMEM((seqs, model), jnp.bfloat16),
            pltpu.VMEM((W_SLOTS, model, W_COLS), jnp.bfloat16),
            pltpu.VMEM(k_cache.shape, k_cache.dtype),
            pltpu.VMEM(v_cache.shape, v_cache.dtype),
            pltpu.VMEM((q_heads * seqs, head_dim), jnp.float32),
            pltpu.VMEM((kv_heads * seqs, head_dim), jnp.float32),
            pltpu.VMEM((kv_heads * seqs, head_dim), jnp.float32),
            pltpu.VMEM((q_heads, 128), jnp.float32),
            pltpu.VMEM((q_heads, 128), jnp.float32),
            pltpu.SemaphoreType.DMA((W_SLOTS,)),
            pltpu.SemaphoreType.DMA((groups,)),
            pltpu.SemaphoreType.DMA((groups,)),
            pltpu.SemaphoreType.DMA((groups,)),
            pltpu.SemaphoreType.DMA((groups,)),
        ],
        compiler_params=pltpu.CompilerParams(vmem_limit_bytes=56 * 1024 * 1024),
    )(positions, tokens, cos_t, sin_t, attn_norm[None, :], q_norm[None, :], k_norm[None, :], w_q, w_k, w_v, k_cache, v_cache)


def combine(pieces, seqs, rows_out, final=False):
    stats = [jnp.transpose(s, (1, 0))[:seqs] for _, s in pieces]
    peak = functools.reduce(jnp.maximum, [t[:, 0:2] for t in stats])
    factors = [jnp.exp(t[:, 0:2] - peak) for t in stats]
    total = functools.reduce(jnp.add, [f * t[:, 2:4] for f, t in zip(factors, stats)])
    outs = []
    for hh in range(2):
        acc = None
        for (o, _), f in zip(pieces, factors):
            term = o[hh * seqs:(hh + 1) * seqs] * f[:, hh:hh + 1]
            acc = term if acc is None else acc + term
        if final:
            acc = acc / total[:, hh:hh + 1]
        outs.append(acc)
    if final:
        return outs, None
    both = jnp.concatenate([peak, total, jnp.zeros((seqs, 4), jnp.float32)], axis=1)
    both = jnp.concatenate([both, jnp.zeros((128 - seqs, 8), jnp.float32)], axis=0)
    return outs, jnp.transpose(both, (1, 0))


def tail_kernel(part_ref, wo_ref, tok_ref, out_ref, mine, pin, acc, rel, fin, att, wov, res,
                psem, wsem, s0, r0, s1, r1, s2, r2, s3, r3, s4, r4):
    seqs, model = tok_ref.shape
    me = lax.axis_index('sp')
    n = lax.axis_size('sp')
    chips = n // 2
    core, chip = lax.rem(me, 2), me // 2
    c_right, c_left, c_opp = lax.rem(chip + 1, chips), lax.rem(chip + chips - 1, chips), lax.rem(chip + 2, chips)
    partner = chip * 2 + 1 - core
    right, left = c_right * 2 + core, c_left * 2 + core
    body = 2 * seqs
    k_rows = wov.shape[1]

    load = pltpu.make_async_copy(part_ref, mine, psem)
    load.start()

    def wo_copy(k):
        return pltpu.make_async_copy(wo_ref.at[pl.ds(pl.multiple_of(k * k_rows, k_rows), k_rows)], wov.at[k], wsem.at[k])

    barrier = pltpu.get_barrier_semaphore()
    for peer in (partner, right, left):
        pl.semaphore_signal(barrier, inc=1, device_id={'sp': peer}, device_id_type=MESH)
    for k in range(wov.shape[0]):
        wo_copy(k).start()
    load.wait()
    pl.semaphore_wait(barrier, 3)

    def send(src, dst, ss, rs, peer):
        copy = pltpu.make_async_remote_copy(src_ref=src, dst_ref=dst, send_sem=ss, recv_sem=rs,
                                            device_id={'sp': peer}, device_id_type=MESH)
        copy.start()
        return copy

    order = (c_opp, c_right, c_left, chip)
    halves = 2 * chips
    sends = []
    pair = []
    for i, c in enumerate(order):
        copy = send(mine.at[pl.ds((1 - core) * halves + 2 * c, 2)], pin.at[i], s0.at[i], r0.at[i], partner)
        pair.append(copy)

    def put(dst, outs, stat):
        for hh in range(2):
            dst[hh * seqs:(hh + 1) * seqs, :] = outs[hh]
        dst[body:body + STAT_ROWS, :] = stat

    def read(ref):
        return ref[0:body, :], ref[body:body + STAT_ROWS, :]

    def merge_pair(i):
        pair[i].wait_recv()
        for h in range(2):
            own = mine.at[core * halves + 2 * order[i] + h]
            put(acc.at[i, h], *combine([read(own), read(pin.at[i, h])], seqs, body))

    merge_pair(0)
    sends.append(send(acc.at[0, 1], rel.at[1], s1.at[1], r1.at[1], right))
    sends.append(send(acc.at[0, 0], rel.at[0], s1.at[0], r1.at[0], left))
    relay_b, relay_a = sends[0], sends[1]
    merge_pair(1)
    fin_left_a = send(acc.at[1, 0], fin.at[0, 0], s2.at[0], r2.at[0], right)
    merge_pair(2)
    fin_right_b = send(acc.at[2, 1], fin.at[1, 1], s2.at[1], r2.at[1], left)
    merge_pair(3)
    relay_b.wait_recv()
    put(fin.at[2, 1], *combine([read(acc.at[1, 1]), read(rel.at[1])], seqs, body))
    fin_left_b = send(fin.at[2, 1], fin.at[0, 1], s2.at[2], r2.at[2], right)
    relay_a.wait_recv()
    put(fin.at[2, 0], *combine([read(acc.at[2, 0]), read(rel.at[0])], seqs, body))
    fin_right_a = send(fin.at[2, 0], fin.at[1, 0], s2.at[3], r2.at[3], left)

    mine_k = core * chips + chip
    for h, (from_left, from_right) in ((0, (fin_left_a, fin_right_a)), (1, (fin_left_b, fin_right_b))):
        from_left.wait_recv()
        from_right.wait_recv()
        outs, _ = combine([read(acc.at[3, h]), read(fin.at[0, h]), read(fin.at[1, h])], seqs, body, final=True)
        for hh in range(2):
            att[mine_k, h, hh * seqs:(hh + 1) * seqs, :] = outs[hh].astype(jnp.bfloat16).astype(jnp.float32)

    k_left, k_right, k_opp = core * chips + c_left, core * chips + c_right, core * chips + c_opp
    o_core = 1 - core
    to_right_b = send(att.at[mine_k, 1], att.at[mine_k, 1], s3.at[0], r3.at[0], right)
    to_left_a = send(att.at[mine_k, 0], att.at[mine_k, 0], s3.at[1], r3.at[1], left)
    to_right_a = send(att.at[mine_k, 0], att.at[mine_k, 0], s3.at[2], r3.at[2], right)
    to_left_b = send(att.at[mine_k, 1], att.at[mine_k, 1], s3.at[3], r3.at[3], left)
    to_partner = send(att.at[mine_k], att.at[mine_k], s3.at[4], r3.at[4], partner)

    cols = 512

    def multiply(k, first=False):
        wo_copy(k).wait()
        lhs = jnp.concatenate([att[k, h, hh * seqs:(hh + 1) * seqs, :] for h in range(2) for hh in range(2)], axis=1)
        lhs = lhs.astype(jnp.bfloat16)

        def tile(i, carry):
            off = pl.ds(pl.multiple_of(i * cols, cols), cols)
            y = jnp.dot(lhs, wov[k, :, off], preferred_element_type=jnp.float32)
            res[:, off] = y if first else res[:, off] + y
            return carry

        lax.fori_loop(0, model // cols, tile, 0)

    multiply(mine_k, first=True)
    to_right_b.wait_recv()
    fwd_right = send(att.at[k_left, 1], att.at[k_left, 1], s4.at[0], r4.at[0], right)
    p1 = send(att.at[k_left, 1], att.at[k_left, 1], s4.at[2], r4.at[2], partner)
    to_left_a.wait_recv()
    fwd_left = send(att.at[k_right, 0], att.at[k_right, 0], s4.at[1], r4.at[1], left)
    p2 = send(att.at[k_right, 0], att.at[k_right, 0], s4.at[3], r4.at[3], partner)
    to_partner.wait_recv()
    multiply(o_core * chips + chip)
    to_right_a.wait_recv()
    p3 = send(att.at[k_left, 0], att.at[k_left, 0], s4.at[4], r4.at[4], partner)
    to_left_b.wait_recv()
    p4 = send(att.at[k_right, 1], att.at[k_right, 1], s4.at[5], r4.at[5], partner)
    multiply(k_left)
    multiply(k_right)
    p1.wait_recv()
    p3.wait_recv()
    multiply(o_core * chips + c_left)
    p2.wait_recv()
    p4.wait_recv()
    multiply(o_core * chips + c_right)
    fwd_right.wait_recv()
    p5 = send(att.at[k_opp, 1], att.at[k_opp, 1], s4.at[6], r4.at[6], partner)
    fwd_left.wait_recv()
    p6 = send(att.at[k_opp, 0], att.at[k_opp, 0], s4.at[7], r4.at[7], partner)
    multiply(k_opp)
    p5.wait_recv()
    p6.wait_recv()
    multiply(o_core * chips + c_opp)
    out_ref[...] = (tok_ref[...].astype(jnp.float32) + res[...]).astype(jnp.bfloat16)
    for copy in pair + sends + [fin_left_a, fin_right_b, fin_left_b, fin_right_a, to_right_b, to_left_a, to_right_a,
                                to_left_b, to_partner, fwd_right, fwd_left, p1, p2, p3, p4, p5, p6]:
        copy.wait_send()


def tail_stage(part, w_o, tokens, group):
    seqs, model = tokens.shape
    halves, rows, head_dim = part.shape
    chips = group // 2
    vmem = pl.BlockSpec(memory_space=pltpu.VMEM)
    anyspec = pl.BlockSpec(memory_space=pl.ANY)
    dma = pltpu.SemaphoreType.DMA
    return pl.pallas_call(
        tail_kernel,
        name='tail_stage',
        out_shape=jax.ShapeDtypeStruct((seqs, model), jnp.bfloat16),
        in_specs=[anyspec, anyspec, vmem],
        out_specs=vmem,
        scratch_shapes=[
            pltpu.VMEM(part.shape, jnp.float32),
            pltpu.VMEM((chips, 2, rows, head_dim), jnp.float32),
            pltpu.VMEM((chips, 2, rows, head_dim), jnp.float32),
            pltpu.VMEM((2, rows, head_dim), jnp.float32),
            pltpu.VMEM((3, 2, rows, head_dim), jnp.float32),
            pltpu.VMEM((group, 2, 2 * seqs, head_dim), jnp.float32),
            pltpu.VMEM((group, w_o.shape[0] // group, model), jnp.bfloat16),
            pltpu.VMEM((seqs, model), jnp.float32),
            dma, dma((group,)),
            dma((chips,)), dma((chips,)), dma((2,)), dma((2,)), dma((4,)), dma((4,)), dma((5,)), dma((5,)), dma((8,)), dma((8,)),
        ],
        compiler_params=pltpu.CompilerParams(collective_id=0, has_side_effects=True, vmem_limit_bytes=56 * 1024 * 1024),
    )(part, w_o, tokens)


def solution(mesh):
    cache_spec = P('dp', 'sp', None, None)
    group = mesh.shape['sp']

    def device_step(tokens, positions, k_cache, v_cache, w_q, w_k, w_v, w_o, attn_norm, q_norm, k_norm):
        cos_t, sin_t = rope_table(positions, q_norm.shape[0])
        k_upd, v_upd, new_kv, part = local_stage(tokens, positions, cos_t, sin_t, k_cache, v_cache, w_q, w_k, w_v, attn_norm, q_norm, k_norm)
        block_out = tail_stage(part, w_o, tokens, group)
        return block_out, k_upd, v_upd, new_kv

    return jax.shard_map(device_step, mesh=mesh, in_specs=(P('dp', None), P('dp'), cache_spec, cache_spec, P(), P(), P(), P(), P(), P(), P()), out_specs=(P('dp', None), cache_spec, cache_spec, P('dp', None, None, None)), check_vma=False)
```

time: 181 us -> 82.1 us (0.45)
  Pallas kernels: 0 us -> 76.3 us
  waiting for transfers between devices: 57.2 us -> 0 us
  matrix products: 45.7 us -> 0 us
  blocking collectives: 26.9 us -> 0 us
  other arithmetic: 22.8 us -> 1.58 us
  between operations: 14.3 us -> 0.65 us
  local copies, waits for them, and re-layouts: 11.8 us -> 3.18 us
    pallas_call x0 -> x2, Pallas kernels: none -> 76.3 us  [the longest x1 43.7 us: local_stage(): pl.pallas_call(local_kernel, name='local_stage', out_shape=(jax.ShapeDtyp...]
    psum x1 -> x0, waiting for transfers between devices: 57.2 us -> none  [device_step(): summed = lax.psum(packed, 'sp')]
    dot_general x6 -> x0, matrix products: 45.7 us -> none  [the longest x1 14.4 us: device_step(): jnp.dot(attn_out, w_o, preferred_element_type=jnp.float32)]
    pmax x1 -> x0, blocking collectives: 26.9 us -> none  [device_step(): global_peak = lax.pmax(local_peak, 'sp')]
    select_n x1 -> x0, other arithmetic: 9.47 us -> none  [local_attention(): v_upd = jnp.where(write_mask, v_new[:, None], v_loc)]
    convert_element_type x4 -> x0, other arithmetic: 3.8 us -> none  [the longest x3 2.02 us: rms_scale(): gain.astype(jnp.float32)]
    reduce_sum x4 -> x0, other arithmetic: 3.22 us -> none  [the longest x3 1.87 us: rms_scale(): jnp.mean(values * values, axis=-1, keepdims=True) + NORM_EPS]
    div x1 -> x0, local copies, waits for them, and re-layouts: 3.11 us -> none  [device_step(): summed[..., :head_dim] / summed[..., head_dim:]]
  transfers between devices with their start and end apart: 1 -> 0, of which waited for: 1 -> 0; matrix products, arithmetic and copies ran while one was open for 0% -> 0% of each run, Pallas kernels for 0% -> 0%
where the time goes in v1:
time: 82.1 us; the launch traced here: 81.7 us
  Pallas kernels  76.3 us (93%)
  local copies, waits for them, and re-layouts  3.18 us (4%)
  other arithmetic  1.58 us (2%)
    pallas_call x1, Pallas kernels, local_stage(): pl.pallas_call(local_kernel, name='local_stage', out_shape=(jax.ShapeDtyp...  43.7 us
    pallas_call x1, Pallas kernels, tail_stage(): pl.pallas_call(tail_kernel, name='tail_stage', out_shape=jax.ShapeDtypeSt...  32.6 us
    unnamed x1, local copies, waits for them, and re-layouts  1.87 us

profile of v1, /device:TPU:113, one launch (start us, length us, event | category | flops | bytes accessed | tf_op | source)
XLA Modules:
  0.0 81.7 jit_solution(5744530020383854843)
XLA Ops:
  0.6 0.7 convert_element_type.3
  1.3 1.3 %broadcast_in_dim.11.an_ref = bf16[1,4096]{1,0:T(2,128)(2,1)} reshape(bf16[4096]{0:T(1024)(128)(2,1)} %param.19) | data formatting | bytes 16384 | tf_op jit(solution)/shard_map/broadcast_in_dim | solution.py:231
  2.6 0.2 fusion
  2.8 0.7 pad_maximum_fusion
  3.5 43.7 %local_stage.1 = (bf16[64,64,8,128]{3,2,1,0:T(8,128)(2,1)}, bf16[64,64,8,128]{3,2,1,0:T(8,128)(2,1)}, bf16[64,2,8,128]{3,2,1,0:T(8,128)(2,1)}, f32[16,136,128]{2,1,0:T(8,128)}) custom-call(s32[64]{0:T(128)} %pos_ref.1, bf16[64,4096]{1,0:T(8,128)(2,1)} %tok_ref.3, f32[64,128]{1,0:T(8,128)} %get-tuple-element.15.cos_ref, f32[64,128]{1,0:T(8,128)} %get-tuple-element.16.sin_ref, ...), custom_call_target="tpu_custom_call" | custom-call | tf_op jit(solution)/shard_map/local_stage/pallas_call | solution.py:203
  47.2 32.6 %tail_stage.1 = bf16[64,4096]{1,0:T(8,128)(2,1)} custom-call(f32[16,136,128]{2,1,0:T(8,128)} %get-tuple-element.8.part_ref, bf16[4096,4096]{1,0:T(8,128)(2,1)} %wo_ref.1, bf16[64,4096]{1,0:T(8,128)(2,1)} %tok_ref.3), custom_call_target="tpu_custom_call" | custom-call | tf_op jit(solution)/shard_map/tail_stage/pallas_call | solution.py:399
  79.8 1.9 %copy.16 = bf16[64,4096]{1,0:T(8,128)(2,1)} copy(bf16[64,4096]{1,0:T(8,128)(2,1)} %tail_stage.1) | data formatting | bytes 1048576
  (1 shorter events, 0.0 us)

commit v2 on v1

--- a/solution.py
+++ b/solution.py
@@ -2,6 +2,7 @@
 
 import jax
 import jax.numpy as jnp
+import numpy as np
 from jax import lax
 from jax.experimental import pallas as pl
 from jax.experimental.pallas import tpu as pltpu
@@ -11,16 +12,14 @@
 ROPE_THETA = 1000000.0
 NEG_FILL = -1e30
 MESH = pl.DeviceIdType.MESH
-W_COLS = 512
-W_SLOTS = 5
+W_ROWS = 512
+W_SLOTS = 3
 STAT_ROWS = 8
 
 
-def rope_table(positions, head_dim):
-    inv_freq = ROPE_THETA ** (-jnp.arange(head_dim // 2, dtype=jnp.float32) * 2.0 / head_dim)
-    angles = positions.astype(jnp.float32)[:, None] * inv_freq[None, :]
-    cos, sin = jnp.cos(angles), jnp.sin(angles)
-    return jnp.concatenate([cos, cos], axis=-1), jnp.concatenate([-sin, sin], axis=-1)
+def rope_frequencies(head_dim):
+    inv_freq = ROPE_THETA ** (-np.arange(head_dim // 2, dtype=np.float64) * 2.0 / head_dim)
+    return np.concatenate([inv_freq, inv_freq])[None, :].astype(np.float32)
 
 
 def norm_rope(proj, gain, cos_full, sin_full):
@@ -31,9 +30,9 @@
     return (normed * cos_full + turned * sin_full).astype(jnp.bfloat16).astype(jnp.float32)
 
 
-def local_kernel(pos_ref, tok_ref, cos_ref, sin_ref, an_ref, qn_ref, kn_ref, wq_ref, wk_ref, wv_ref, kc_ref, vc_ref,
-                 ko_ref, vo_ref, new_ref, part_ref,
-                 hid, wbuf, kbuf, vbuf, qf, kf, vf, mstat, lstat, wsem, ksem, vsem, kosem, vosem):
+def local_kernel(pos_in, tok_in, freq_in, an_in, qn_in, kn_in, wq_ref, wk_ref, wv_ref, kc_ref, vc_ref,
+                 ko_ref, vo_ref, new_out, part_ref,
+                 pos_ref, tok_ref, freq_ref, an_ref, qn_ref, kn_ref, new_ref, insem, newsem, hid, wqb, wkb, wvb, yq, yk, yv, cosb, sinb, kbuf, vbuf, qf, kf, vf, mstat, lstat, wsem, ksem, vsem, kosem, vosem):
     seqs, model = tok_ref.shape
     head_dim = qn_ref.shape[-1]
     slots, kv_heads = kbuf.shape[1], kbuf.shape[2]
@@ -41,87 +40,84 @@
     per_group = seqs // groups
     q_heads = wq_ref.shape[1] // head_dim
     start = lax.axis_index('sp') * slots
-    n_k = wk_ref.shape[1] // W_COLS
-    n_q = wq_ref.shape[1] // W_COLS
-    n_all = 2 * n_k + n_q
-    heads_per = W_COLS // head_dim
-
-    def w_copy(ref, col, n):
-        slot = n % W_SLOTS if isinstance(n, int) else lax.rem(n, W_SLOTS)
-        off = col * W_COLS if isinstance(col, int) else pl.multiple_of(col * W_COLS, W_COLS)
-        return pltpu.make_async_copy(ref.at[:, pl.ds(off, W_COLS)], wbuf.at[slot], wsem.at[slot])
-
-    def w_start(n):
-        if n < n_k:
-            w_copy(wk_ref, n, n).start()
-        elif n < 2 * n_k:
-            w_copy(wv_ref, n - n_k, n).start()
-        else:
-            w_copy(wq_ref, n - 2 * n_k, n).start()
+    steps = model // W_ROWS
+    weights = ((wk_ref, wkb, yk), (wv_ref, wvb, yv), (wq_ref, wqb, yq))
+
+    def w_copies(i):
+        slot = lax.rem(i, W_SLOTS)
+        rows = pl.ds(pl.multiple_of(i * W_ROWS, W_ROWS), W_ROWS)
+        return [pltpu.make_async_copy(ref.at[rows], buf.at[slot], wsem.at[j, slot]) for j, (ref, buf, _) in enumerate(weights)]
 
     def cache_in(ref, buf, sem, g):
         rows = pl.ds(g * per_group, per_group)
         return pltpu.make_async_copy(ref.at[rows], buf.at[rows], sem.at[g])
 
+    smalls = [pltpu.make_async_copy(src, dst, insem.at[j]) for j, (src, dst) in enumerate((
+        (tok_in, tok_ref), (pos_in, pos_ref), (freq_in, freq_ref), (an_in, an_ref), (qn_in, qn_ref), (kn_in, kn_ref)))]
+    for copy in smalls:
+        copy.start()
     for n in range(W_SLOTS):
-        w_start(n)
-
-    blk = 512
+        for copy in w_copies(jnp.int32(n)):
+            copy.start()
+    for copy in smalls:
+        copy.wait()
+
+    lanes = an_ref.shape[1]
     total = jnp.zeros((seqs, 1), jnp.float32)
-    for i in range(model // blk):
-        xf = tok_ref[:, i * blk:(i + 1) * blk].astype(jnp.float32)
+    for i in range(model // lanes):
+        xf = tok_ref[:, i * lanes:(i + 1) * lanes].astype(jnp.float32)
         total = total + jnp.sum(xf * xf, axis=-1, keepdims=True)
     inv = lax.rsqrt(total / model + NORM_EPS)
-    for i in range(model // blk):
-        xf = tok_ref[:, i * blk:(i + 1) * blk].astype(jnp.float32)
-        gain = an_ref[:, i * blk:(i + 1) * blk].astype(jnp.float32)
-        hid[:, i * blk:(i + 1) * blk] = (xf * inv * gain).astype(jnp.bfloat16)
-
-    cos_full, sin_full = cos_ref[...], sin_ref[...]
-
-    def project(n):
-        slot = n % W_SLOTS if isinstance(n, int) else lax.rem(n, W_SLOTS)
-        w_copy(wq_ref, 0, n).wait()
-        return jnp.dot(hid[...], wbuf[slot], preferred_element_type=jnp.float32)
-
-    k_gain = kn_ref[...].astype(jnp.float32)
-    q_gain = qn_ref[...].astype(jnp.float32)
-    for n in range(2 * n_k):
-        y = project(n)
-        if n + W_SLOTS < n_all:
-            w_start(n + W_SLOTS)
-        for hh in range(heads_per):
-            piece = y[:, hh * head_dim:(hh + 1) * head_dim]
-            if n < n_k:
-                row = (n * heads_per + hh) * seqs
-                kf[row:row + seqs, :] = norm_rope(piece, k_gain, cos_full, sin_full)
-            else:
-                row = ((n - n_k) * heads_per + hh) * seqs
-                vf[row:row + seqs, :] = piece.astype(jnp.bfloat16).astype(jnp.float32)
-
-    def q_step(i, carry):
-        n = i + 2 * n_k
-        y = project(n)
-
-        @pl.when(n + W_SLOTS < n_all)
+    per_step = W_ROWS // lanes
+    for i in range(model // lanes):
+        xf = tok_ref[:, i * lanes:(i + 1) * lanes].astype(jnp.float32)
+        gain = an_ref[i:i + 1, :].astype(jnp.float32)
+        hid[i // per_step, :, (i % per_step) * lanes:(i % per_step + 1) * lanes] = (xf * inv * gain).astype(jnp.bfloat16)
+
+    for b in range(seqs):
+        cosb[b:b + 1, :] = jnp.full((1, head_dim), pos_ref[b], jnp.int32).astype(jnp.float32)
+    angles = cosb[...] * freq_ref[...]
+    sign = jnp.where(lax.broadcasted_iota(jnp.int32, angles.shape, 1) < head_dim // 2, -1.0, 1.0)
+    sinb[...] = jnp.sin(angles) * sign
+    cosb[...] = jnp.cos(angles)
+    for y in (yq, yk, yv):
+        y[...] = jnp.zeros_like(y)
+
+    def w_step(i, carry):
+        slot = lax.rem(i, W_SLOTS)
+        lhs = hid[i]
+        for copy, (_, buf, y) in zip(w_copies(i), weights):
+            copy.wait()
+            y[...] += jnp.dot(lhs, buf[slot], preferred_element_type=jnp.float32)
+
+        @pl.when(i + W_SLOTS < steps)
         def _():
-            w_copy(wq_ref, i + W_SLOTS, n + W_SLOTS).start()
-
-        @pl.when(n + W_SLOTS >= n_all)
+            for copy in w_copies(i + W_SLOTS):
+                copy.start()
+
+        @pl.when(i + W_SLOTS >= steps)
         def _():
-            g = n + W_SLOTS - n_all
+            g = i + W_SLOTS - steps
             cache_in(kc_ref, kbuf, ksem, g).start()
             cache_in(vc_ref, vbuf, vsem, g).start()
 
-        for hh in range(heads_per):
-            row = pl.multiple_of(i * (heads_per * seqs) + hh * seqs, seqs)
-            qf[pl.ds(row, seqs), :] = norm_rope(y[:, hh * head_dim:(hh + 1) * head_dim], q_gain, cos_full, sin_full)
         return carry
 
-    lax.fori_loop(0, n_q, q_step, 0)
+    lax.fori_loop(0, steps, w_step, 0)
     for g in range(W_SLOTS, groups):
         cache_in(kc_ref, kbuf, ksem, g).start()
         cache_in(vc_ref, vbuf, vsem, g).start()
+
+    cos_full, sin_full = cosb[...], sinb[...]
+    k_gain = kn_ref[...].astype(jnp.float32)
+    q_gain = qn_ref[...].astype(jnp.float32)
+    for h in range(kv_heads):
+        cols = slice(h * head_dim, (h + 1) * head_dim)
+        rows = slice(h * seqs, (h + 1) * seqs)
+        kf[rows, :] = norm_rope(yk[:, cols], k_gain, cos_full, sin_full)
+        vf[rows, :] = yv[:, cols].astype(jnp.bfloat16).astype(jnp.float32)
+    for h in range(q_heads):
+        qf[h * seqs:(h + 1) * seqs, :] = norm_rope(yq[:, h * head_dim:(h + 1) * head_dim], q_gain, cos_full, sin_full)
 
     half = q_heads // 2
     cols = slots * kv_heads
@@ -175,6 +171,7 @@
         rows = pl.ds(g * per_group, per_group)
         pltpu.make_async_copy(kbuf.at[rows], ko_ref.at[rows], kosem.at[g]).start()
         pltpu.make_async_copy(vbuf.at[rows], vo_ref.at[rows], vosem.at[g]).start()
+        pltpu.make_async_copy(new_ref.at[rows], new_out.at[rows], newsem.at[g]).start()
         return carry
 
     lax.fori_loop(0, groups, group_step, 0)
@@ -190,15 +187,21 @@
         rows = pl.ds(g * per_group, per_group)
         pltpu.make_async_copy(kbuf.at[rows], ko_ref.at[rows], kosem.at[g]).wait()
         pltpu.make_async_copy(vbuf.at[rows], vo_ref.at[rows], vosem.at[g]).wait()
-
-
-def local_stage(tokens, positions, cos_t, sin_t, k_cache, v_cache, w_q, w_k, w_v, attn_norm, q_norm, k_norm):
+        pltpu.make_async_copy(new_ref.at[rows], new_out.at[rows], newsem.at[g]).wait()
+
+
+def in_hbm(*arrays):
+    return [pltpu.with_memory_space_constraint(jnp.asarray(a), pltpu.HBM) for a in arrays]
+
+
+def local_stage(tokens, positions, k_cache, v_cache, w_q, w_k, w_v, attn_norm, q_norm, k_norm):
     seqs, model = tokens.shape
     slots, kv_heads, head_dim = k_cache.shape[1:]
     q_heads = w_q.shape[1] // head_dim
     groups = 8
     vmem = pl.BlockSpec(memory_space=pltpu.VMEM)
     anyspec = pl.BlockSpec(memory_space=pl.ANY)
+    hbm = pl.BlockSpec(memory_space=pltpu.HBM)
     part_shape = (q_heads // 2, 2 * seqs + STAT_ROWS, head_dim)
     return pl.pallas_call(
         local_kernel,
@@ -207,13 +210,29 @@
             jax.ShapeDtypeStruct(k_cache.shape, k_cache.dtype),
             jax.ShapeDtypeStruct(v_cache.shape, v_cache.dtype),
             jax.ShapeDtypeStruct((seqs, 2, kv_heads, head_dim), jnp.bfloat16),
-            jax.ShapeDtypeStruct(part_shape, jnp.float32),
+            pltpu.VMEM(part_shape, jnp.float32),
         ),
-        in_specs=[pl.BlockSpec(memory_space=pltpu.SMEM)] + [vmem] * 6 + [anyspec] * 5,
-        out_specs=(anyspec, anyspec, vmem, vmem),
+        in_specs=[hbm] * 11,
+        out_specs=(anyspec, anyspec, anyspec, vmem),
         scratch_shapes=[
-            pltpu.VMEM((seqs, model), jnp.bfloat16),
-            pltpu.VMEM((W_SLOTS, model, W_COLS), jnp.bfloat16),
+            pltpu.SMEM(positions.shape, jnp.int32),
+            pltpu.VMEM(tokens.shape, tokens.dtype),
+            pltpu.VMEM((1, head_dim), jnp.float32),
+            pltpu.VMEM((model // 128, 128), attn_norm.dtype),
+            pltpu.VMEM((1, head_dim), q_norm.dtype),
+            pltpu.VMEM((1, head_dim), k_norm.dtype),
+            pltpu.VMEM((seqs, 2, kv_heads, head_dim), jnp.bfloat16),
+            pltpu.SemaphoreType.DMA((6,)),
+            pltpu.SemaphoreType.DMA((groups,)),
+            pltpu.VMEM((model // W_ROWS, seqs, W_ROWS), jnp.bfloat16),
+            pltpu.VMEM((W_SLOTS, W_ROWS, w_q.shape[1]), jnp.bfloat16),
+            pltpu.VMEM((W_SLOTS, W_ROWS, w_k.shape[1]), jnp.bfloat16),
+            pltpu.VMEM((W_SLOTS, W_ROWS, w_v.shape[1]), jnp.bfloat16),
+            pltpu.VMEM((seqs, w_q.shape[1]), jnp.float32),
+            pltpu.VMEM((seqs, w_k.shape[1]), jnp.float32),
+            pltpu.VMEM((seqs, w_v.shape[1]), jnp.float32),
+            pltpu.VMEM((seqs, head_dim), jnp.float32),
+            pltpu.VMEM((seqs, head_dim), jnp.float32),
             pltpu.VMEM(k_cache.shape, k_cache.dtype),
             pltpu.VMEM(v_cache.shape, v_cache.dtype),
             pltpu.VMEM((q_heads * seqs, head_dim), jnp.float32),
@@ -221,14 +240,14 @@
             pltpu.VMEM((kv_heads * seqs, head_dim), jnp.float32),
             pltpu.VMEM((q_heads, 128), jnp.float32),
             pltpu.VMEM((q_heads, 128), jnp.float32),
-            pltpu.SemaphoreType.DMA((W_SLOTS,)),
+            pltpu.SemaphoreType.DMA((3, W_SLOTS)),
             pltpu.SemaphoreType.DMA((groups,)),
             pltpu.SemaphoreType.DMA((groups,)),
             pltpu.SemaphoreType.DMA((groups,)),
             pltpu.SemaphoreType.DMA((groups,)),
         ],
-        compiler_params=pltpu.CompilerParams(vmem_limit_bytes=56 * 1024 * 1024),
-    )(positions, tokens, cos_t, sin_t, attn_norm[None, :], q_norm[None, :], k_norm[None, :], w_q, w_k, w_v, k_cache, v_cache)
+        compiler_params=pltpu.CompilerParams(vmem_limit_bytes=46 * 1024 * 1024),
+    )(*in_hbm(positions, tokens, rope_frequencies(head_dim), attn_norm.reshape(-1, 128), q_norm[None, :], k_norm[None, :]), w_q, w_k, w_v, k_cache, v_cache)
 
 
 def combine(pieces, seqs, rows_out, final=False):
@@ -252,9 +271,11 @@
     return outs, jnp.transpose(both, (1, 0))
 
 
-def tail_kernel(part_ref, wo_ref, tok_ref, out_ref, mine, pin, acc, rel, fin, att, wov, res,
-                psem, wsem, s0, r0, s1, r1, s2, r2, s3, r3, s4, r4):
+def tail_kernel(mine, wo_ref, tok_in, out_ref, tok_ref, toksem, pin, acc, rel, fin, att, wov, res,
+                wsem, s0, r0, s1, r1, s2, r2, s3, r3, s4, r4):
     seqs, model = tok_ref.shape
+    tok_copy = pltpu.make_async_copy(tok_in, tok_ref, toksem)
+    tok_copy.start()
     me = lax.axis_index('sp')
     n = lax.axis_size('sp')
     chips = n // 2
@@ -265,18 +286,12 @@
     body = 2 * seqs
     k_rows = wov.shape[1]
 
-    load = pltpu.make_async_copy(part_ref, mine, psem)
-    load.start()
-
     def wo_copy(k):
         return pltpu.make_async_copy(wo_ref.at[pl.ds(pl.multiple_of(k * k_rows, k_rows), k_rows)], wov.at[k], wsem.at[k])
 
     barrier = pltpu.get_barrier_semaphore()
     for peer in (partner, right, left):
         pl.semaphore_signal(barrier, inc=1, device_id={'sp': peer}, device_id_type=MESH)
-    for k in range(wov.shape[0]):
-        wo_copy(k).start()
-    load.wait()
     pl.semaphore_wait(barrier, 3)
 
     def send(src, dst, ss, rs, peer):
@@ -293,6 +308,9 @@
         copy = send(mine.at[pl.ds((1 - core) * halves + 2 * c, 2)], pin.at[i], s0.at[i], r0.at[i], partner)
         pair.append(copy)
 
+    for k in range(2):
+        wo_copy(k).start()
+
     def put(dst, outs, stat):
         for hh in range(2):
             dst[hh * seqs:(hh + 1) * seqs, :] = outs[hh]
@@ -311,11 +329,15 @@
     sends.append(send(acc.at[0, 1], rel.at[1], s1.at[1], r1.at[1], right))
     sends.append(send(acc.at[0, 0], rel.at[0], s1.at[0], r1.at[0], left))
     relay_b, relay_a = sends[0], sends[1]
+    for k in range(2, 4):
+        wo_copy(k).start()
     merge_pair(1)
     fin_left_a = send(acc.at[1, 0], fin.at[0, 0], s2.at[0], r2.at[0], right)
     merge_pair(2)
     fin_right_b = send(acc.at[2, 1], fin.at[1, 1], s2.at[1], r2.at[1], left)
     merge_pair(3)
+    for k in range(4, 8):
+        wo_copy(k).start()
     relay_b.wait_recv()
     put(fin.at[2, 1], *combine([read(acc.at[1, 1]), read(rel.at[1])], seqs, body))
     fin_left_b = send(fin.at[2, 1], fin.at[0, 1], s2.at[2], r2.at[2], right)
@@ -383,6 +405,7 @@
     p5.wait_recv()
     p6.wait_recv()
     multiply(o_core * chips + c_opp)
+    tok_copy.wait()
     out_ref[...] = (tok_ref[...].astype(jnp.float32) + res[...]).astype(jnp.bfloat16)
     for copy in pair + sends + [fin_left_a, fin_right_b, fin_left_b, fin_right_a, to_right_b, to_left_a, to_right_a,
                                 to_left_b, to_partner, fwd_right, fwd_left, p1, p2, p3, p4, p5, p6]:
@@ -394,16 +417,17 @@
     halves, rows, head_dim = part.shape
     chips = group // 2
     vmem = pl.BlockSpec(memory_space=pltpu.VMEM)
-    anyspec = pl.BlockSpec(memory_space=pl.ANY)
+    hbm = pl.BlockSpec(memory_space=pltpu.HBM)
     dma = pltpu.SemaphoreType.DMA
     return pl.pallas_call(
         tail_kernel,
         name='tail_stage',
-        out_shape=jax.ShapeDtypeStruct((seqs, model), jnp.bfloat16),
-        in_specs=[anyspec, anyspec, vmem],
+        out_shape=pltpu.VMEM((seqs, model), jnp.bfloat16),
+        in_specs=[vmem, hbm, hbm],
         out_specs=vmem,
         scratch_shapes=[
-            pltpu.VMEM(part.shape, jnp.float32),
+            pltpu.VMEM((seqs, model), tokens.dtype),
+            dma,
             pltpu.VMEM((chips, 2, rows, head_dim), jnp.float32),
             pltpu.VMEM((chips, 2, rows, head_dim), jnp.float32),
             pltpu.VMEM((2, rows, head_dim), jnp.float32),
@@ -411,11 +435,11 @@
             pltpu.VMEM((group, 2, 2 * seqs, head_dim), jnp.float32),
             pltpu.VMEM((group, w_o.shape[0] // group, model), jnp.bfloat16),
             pltpu.VMEM((seqs, model), jnp.float32),
-            dma, dma((group,)),
+            dma((group,)),
             dma((chips,)), dma((chips,)), dma((2,)), dma((2,)), dma((4,)), dma((4,)), dma((5,)), dma((5,)), dma((8,)), dma((8,)),
         ],
-        compiler_params=pltpu.CompilerParams(collective_id=0, has_side_effects=True, vmem_limit_bytes=56 * 1024 * 1024),
-    )(part, w_o, tokens)
+        compiler_params=pltpu.CompilerParams(collective_id=0, has_side_effects=True, vmem_limit_bytes=44 * 1024 * 1024),
+    )(part, *in_hbm(w_o, tokens))
 
 
 def solution(mesh):
@@ -423,8 +447,7 @@
     group = mesh.shape['sp']
 
     def device_step(tokens, positions, k_cache, v_cache, w_q, w_k, w_v, w_o, attn_norm, q_norm, k_norm):
-        cos_t, sin_t = rope_table(positions, q_norm.shape[0])
-        k_upd, v_upd, new_kv, part = local_stage(tokens, positions, cos_t, sin_t, k_cache, v_cache, w_q, w_k, w_v, attn_norm, q_norm, k_norm)
+        k_upd, v_upd, new_kv, part = local_stage(tokens, positions, k_cache, v_cache, w_q, w_k, w_v, attn_norm, q_norm, k_norm)
         block_out = tail_stage(part, w_o, tokens, group)
         return block_out, k_upd, v_upd, new_kv
 

time: 82.1 us -> 79.1 us (0.963)
  local copies, waits for them, and re-layouts: 3.18 us -> 0.8 us
  other arithmetic: 1.58 us -> 0 us
  Pallas kernels: 76.3 us -> 77.5 us
    pallas_call x1, Pallas kernels: 43.7 us -> 46.9 us  [local_stage(): pl.pallas_call(local_kernel, name='local_stage', out_shape=(jax.ShapeDtyp...]
    pallas_call x1, Pallas kernels: 32.6 us -> 30.6 us  [tail_stage(): pl.pallas_call(tail_kernel, name='tail_stage', out_shape=pltpu.VMEM((seqs...]
    broadcast_in_dim x1 -> x0, local copies, waits for them, and re-layouts: 1.31 us -> none  [local_stage(): attn_norm[None, :]]
    unnamed x1, local copies, waits for them, and re-layouts: 1.87 us -> 0.8 us
where the time goes in v2:
time: 79.1 us; the launch traced here: 78.9 us
  Pallas kernels  77.5 us (98%)
  local copies, waits for them, and re-layouts  0.8 us (1%)
    pallas_call x1, Pallas kernels, local_stage(): pl.pallas_call(local_kernel, name='local_stage', out_shape=(jax.ShapeDtyp...  46.9 us
    pallas_call x1, Pallas kernels, tail_stage(): pl.pallas_call(tail_kernel, name='tail_stage', out_shape=pltpu.VMEM((seqs...  30.6 us

profile of v2, /device:TPU:113, one launch (start us, length us, event | category | flops | bytes accessed | tf_op | source)
XLA Modules:
  0.0 78.9 jit_solution(11554847453023282826)
XLA Ops:
  0.6 46.9 %local_stage.1 = (bf16[64,64,8,128]{3,2,1,0:T(8,128)(2,1)}, bf16[64,64,8,128]{3,2,1,0:T(8,128)(2,1)}, bf16[64,2,8,128]{3,2,1,0:T(8,128)(2,1)}, f32[16,136,128]{2,1,0:T(8,128)S(1)}) custom-call(s32[64]{0:T(128)} %pos_in.1, bf16[64,4096]{1,0:T(8,128)(2,1)} %tok_in.3, f32[1,128]{1,0:T(1,128)} %constant.2.clone.freq_in, bf16[32,128]{1,0:T(8,128)(2,1)} %bitcast.3, ...), custom_call_target="tpu_custom_call" | custom-call | tf_op jit(solution)/shard_map/local_stage/pallas_call | solution.py:206
  47.5 30.6 %tail_stage.1 = bf16[64,4096]{1,0:T(8,128)(2,1)S(1)} custom-call(f32[16,136,128]{2,1,0:T(8,128)S(1)} %get-tuple-element.8.mine, bf16[4096,4096]{1,0:T(8,128)(2,1)} %wo_ref.1, bf16[64,4096]{1,0:T(8,128)(2,1)} %tok_in.3), custom_call_target="tpu_custom_call" | custom-call | tf_op jit(solution)/shard_map/tail_stage/pallas_call | solution.py:422
  78.1 0.8 %copy.17 = bf16[64,4096]{1,0:T(8,128)(2,1)} copy(bf16[64,4096]{1,0:T(8,128)(2,1)S(1)} %tail_stage.1) | data formatting | bytes 1048576

commit v3 on v2

--- a/solution.py
+++ b/solution.py
@@ -32,7 +32,7 @@
 
 def local_kernel(pos_in, tok_in, freq_in, an_in, qn_in, kn_in, wq_ref, wk_ref, wv_ref, kc_ref, vc_ref,
                  ko_ref, vo_ref, new_out, part_ref,
-                 pos_ref, tok_ref, freq_ref, an_ref, qn_ref, kn_ref, new_ref, insem, newsem, hid, wqb, wkb, wvb, yq, yk, yv, cosb, sinb, kbuf, vbuf, qf, kf, vf, mstat, lstat, wsem, ksem, vsem, kosem, vosem):
+                 pos_ref, tok_ref, freq_ref, an_ref, qn_ref, kn_ref, new_ref, insem, newsem, hid, wqb, wkb, wvb, yq, yk, yv, cosb, sinb, kbuf, vbuf, qf, kf, vf, mstat, lstat, sbuf, ebuf, obuf, wsem, ksem, vsem, kosem, vosem):
     seqs, model = tok_ref.shape
     head_dim = qn_ref.shape[-1]
     slots, kv_heads = kbuf.shape[1], kbuf.shape[2]
@@ -136,36 +136,38 @@
         cache_in(kc_ref, kbuf, ksem, g).wait()
         cache_in(vc_ref, vbuf, vsem, g).wait()
         m_acc, l_acc = mstat[...], lstat[...]
-        for bb in range(per_group):
-            b = g * per_group + bb
+        members = [g * per_group + bb for bb in range(per_group)]
+        for b in members:
             local = pos_ref[b] - start
-            k_new = kf[pl.ds(b, kv_heads, stride=seqs), :].astype(jnp.bfloat16)
-            v_new = vf[pl.ds(b, kv_heads, stride=seqs), :].astype(jnp.bfloat16)
-            new_ref[b, 0] = k_new
-            new_ref[b, 1] = v_new
-
-            @pl.when((local >= 0) & (local < slots))
-            def _():
-                kbuf[b, local] = k_new
-                vbuf[b, local] = v_new
-
+            here = (local >= 0) & (local < slots)
+            at = jnp.clip(local, 0, slots - 1)
+            k_new = kf[pl.ds(b, kv_heads, stride=seqs), :]
+            v_new = vf[pl.ds(b, kv_heads, stride=seqs), :]
+            new_ref[b, 0] = k_new.astype(jnp.bfloat16)
+            new_ref[b, 1] = v_new.astype(jnp.bfloat16)
+            kbuf[b, at] = jnp.where(here, k_new, kbuf[b, at].astype(jnp.float32)).astype(jnp.bfloat16)
+            vbuf[b, at] = jnp.where(here, v_new, vbuf[b, at].astype(jnp.float32)).astype(jnp.bfloat16)
+        for bb, b in enumerate(members):
             q_even = qf[pl.ds(b, half, stride=2 * seqs), :]
             q_odd = qf[pl.ds(b + seqs, half, stride=2 * seqs), :]
             q_b = jnp.concatenate([q_even, q_odd], axis=0).astype(jnp.bfloat16)
             k_b = kbuf[b].reshape(cols, head_dim)
-            v_b = vbuf[b].reshape(cols, head_dim)
-            s = lax.dot_general(q_b, k_b, (((1,), (1,)), ((), ())), preferred_element_type=jnp.float32) * score_scale
-            live = slot_key <= local
-            s = jnp.where(live, s, NEG_FILL)
+            sbuf[bb] = lax.dot_general(q_b, k_b, (((1,), (1,)), ((), ())), preferred_element_type=jnp.float32)
+        for bb, b in enumerate(members):
+            live = slot_key <= pos_ref[b] - start
+            s = jnp.where(live, sbuf[bb] * score_scale, NEG_FILL)
             m = jnp.max(s, axis=-1, keepdims=True)
             e = jnp.where(live, jnp.exp(s - m), 0.0)
             l = jnp.sum(e, axis=-1, keepdims=True)
-            o = jnp.dot(e.astype(jnp.bfloat16), v_b, preferred_element_type=jnp.float32)
+            ebuf[bb] = e.astype(jnp.bfloat16)
+            m_acc = jnp.where(lane == b, m, m_acc)
+            l_acc = jnp.where(lane == b, l, l_acc)
+        for bb, b in enumerate(members):
+            obuf[bb] = jnp.dot(ebuf[bb], vbuf[b].reshape(cols, head_dim), preferred_element_type=jnp.float32)
+        for bb, b in enumerate(members):
             for par in range(2):
                 for i in range(half):
-                    part_ref[i, pl.ds(b + par * seqs, 1), :] = o[par * half + i:par * half + i + 1, :]
-            m_acc = jnp.where(lane == b, m, m_acc)
-            l_acc = jnp.where(lane == b, l, l_acc)
+                    part_ref[i, pl.ds(b + par * seqs, 1), :] = obuf[bb, par * half + i:par * half + i + 1, :]
         mstat[...] = m_acc
         lstat[...] = l_acc
         rows = pl.ds(g * per_group, per_group)
@@ -240,6 +242,9 @@
             pltpu.VMEM((kv_heads * seqs, head_dim), jnp.float32),
             pltpu.VMEM((q_heads, 128), jnp.float32),
             pltpu.VMEM((q_heads, 128), jnp.float32),
+            pltpu.VMEM((seqs // groups, q_heads, slots * kv_heads), jnp.float32),
+            pltpu.VMEM((seqs // groups, q_heads, slots * kv_heads), jnp.bfloat16),
+            pltpu.VMEM((seqs // groups, q_heads, head_dim), jnp.float32),
             pltpu.SemaphoreType.DMA((3, W_SLOTS)),
             pltpu.SemaphoreType.DMA((groups,)),
             pltpu.SemaphoreType.DMA((groups,)),
@@ -368,13 +373,10 @@
         lhs = jnp.concatenate([att[k, h, hh * seqs:(hh + 1) * seqs, :] for h in range(2) for hh in range(2)], axis=1)
         lhs = lhs.astype(jnp.bfloat16)
 
-        def tile(i, carry):
-            off = pl.ds(pl.multiple_of(i * cols, cols), cols)
+        for i in range(model // cols):
+            off = slice(i * cols, (i + 1) * cols)
             y = jnp.dot(lhs, wov[k, :, off], preferred_element_type=jnp.float32)
             res[:, off] = y if first else res[:, off] + y
-            return carry
-
-        lax.fori_loop(0, model // cols, tile, 0)
 
     multiply(mine_k, first=True)
     to_right_b.wait_recv()

time: 79.1 us -> 56.8 us (0.72)
  Pallas kernels: 77.5 us -> 55.3 us
    pallas_call x1, Pallas kernels: 46.9 us -> 30.3 us  [local_stage(): pl.pallas_call(local_kernel, name='local_stage', out_shape=(jax.ShapeDtyp...]
    pallas_call x1, Pallas kernels: 30.6 us -> 25 us  [tail_stage(): pl.pallas_call(tail_kernel, name='tail_stage', out_shape=pltpu.VMEM((seqs...]
where the time goes in v3:
time: 56.8 us
  Pallas kernels  55.3 us (97%)
  local copies, waits for them, and re-layouts  0.8 us (1%)
  between operations  0.65 us (1%)
    pallas_call x1, Pallas kernels, local_stage(): pl.pallas_call(local_kernel, name='local_stage', out_shape=(jax.ShapeDtyp...  30.3 us
    pallas_call x1, Pallas kernels, tail_stage(): pl.pallas_call(tail_kernel, name='tail_stage', out_shape=pltpu.VMEM((seqs...  25 us

profile of v3, /device:TPU:113, one launch (start us, length us, event | category | flops | bytes accessed | tf_op | source)
XLA Modules:
  0.0 56.8 jit_solution(264109298078572108)
XLA Ops:
  0.6 30.3 %local_stage.1 = (bf16[64,64,8,128]{3,2,1,0:T(8,128)(2,1)}, bf16[64,64,8,128]{3,2,1,0:T(8,128)(2,1)}, bf16[64,2,8,128]{3,2,1,0:T(8,128)(2,1)}, f32[16,136,128]{2,1,0:T(8,128)S(1)}) custom-call(s32[64]{0:T(128)} %pos_in.1, bf16[64,4096]{1,0:T(8,128)(2,1)} %tok_in.3, f32[1,128]{1,0:T(1,128)} %constant.2.clone.freq_in, bf16[32,128]{1,0:T(8,128)(2,1)} %bitcast.3, ...), custom_call_target="tpu_custom_call" | custom-call | tf_op jit(solution)/shard_map/local_stage/pallas_call | solution.py:208
  31.0 25.0 %tail_stage.1 = bf16[64,4096]{1,0:T(8,128)(2,1)S(1)} custom-call(f32[16,136,128]{2,1,0:T(8,128)S(1)} %get-tuple-element.8.mine, bf16[4096,4096]{1,0:T(8,128)(2,1)} %wo_ref.1, bf16[64,4096]{1,0:T(8,128)(2,1)} %tok_in.3), custom_call_target="tpu_custom_call" | custom-call | tf_op jit(solution)/shard_map/tail_stage/pallas_call | solution.py:424
  56.0 0.8 %copy.17 = bf16[64,4096]{1,0:T(8,128)(2,1)} copy(bf16[64,4096]{1,0:T(8,128)(2,1)S(1)} %tail_stage.1) | data formatting | bytes 1048576

commit v4 on v3

--- a/solution.py
+++ b/solution.py
@@ -12,9 +12,11 @@
 ROPE_THETA = 1000000.0
 NEG_FILL = -1e30
 MESH = pl.DeviceIdType.MESH
-W_ROWS = 512
-W_SLOTS = 3
 STAT_ROWS = 8
+
+
+def in_hbm(*arrays):
+    return [pltpu.with_memory_space_constraint(jnp.asarray(a), pltpu.HBM) for a in arrays]
 
 
 def rope_frequencies(head_dim):
@@ -30,49 +32,78 @@
     return (normed * cos_full + turned * sin_full).astype(jnp.bfloat16).astype(jnp.float32)
 
 
-def local_kernel(pos_in, tok_in, freq_in, an_in, qn_in, kn_in, wq_ref, wk_ref, wv_ref, kc_ref, vc_ref,
-                 ko_ref, vo_ref, new_out, part_ref,
-                 pos_ref, tok_ref, freq_ref, an_ref, qn_ref, kn_ref, new_ref, insem, newsem, hid, wqb, wkb, wvb, yq, yk, yv, cosb, sinb, kbuf, vbuf, qf, kf, vf, mstat, lstat, sbuf, ebuf, obuf, wsem, ksem, vsem, kosem, vosem):
+def ring_place():
+    me = lax.axis_index('sp')
+    chips = lax.axis_size('sp') // 2
+    core, chip = lax.rem(me, 2), me // 2
+    c_right, c_left, c_opp = lax.rem(chip + 1, chips), lax.rem(chip + chips - 1, chips), lax.rem(chip + 2, chips)
+    return chips, core, chip, c_right, c_left, c_opp, chip * 2 + 1 - core, c_right * 2 + core, c_left * 2 + core
+
+
+def enter(peers):
+    barrier = pltpu.get_barrier_semaphore()
+    for peer in peers:
+        pl.semaphore_signal(barrier, inc=1, device_id={'sp': peer}, device_id_type=MESH)
+    return lambda: pl.semaphore_wait(barrier, len(peers))
+
+
+def send(src, dst, ss, rs, peer):
+    copy = pltpu.make_async_remote_copy(src_ref=src, dst_ref=dst, send_sem=ss, recv_sem=rs,
+                                        device_id={'sp': peer}, device_id_type=MESH)
+    copy.start()
+    return copy
+
+
+def project_kernel(pos_in, tok_in, freq_in, an_in, qn_in, kn_in, wq_ref, wk_ref, wv_ref, kc_ref, vc_ref,
+                   qf, kf, vf, kbuf, vbuf,
+                   pos_ref, tok_ref, freq_ref, an_ref, qn_ref, kn_ref, hid, wbuf, cosb, sinb, insem, wsem, csem, ss, rs):
     seqs, model = tok_ref.shape
     head_dim = qn_ref.shape[-1]
-    slots, kv_heads = kbuf.shape[1], kbuf.shape[2]
-    groups = ksem.shape[0]
-    per_group = seqs // groups
-    q_heads = wq_ref.shape[1] // head_dim
-    start = lax.axis_index('sp') * slots
-    steps = model // W_ROWS
-    weights = ((wk_ref, wkb, yk), (wv_ref, wvb, yv), (wq_ref, wqb, yq))
-
-    def w_copies(i):
-        slot = lax.rem(i, W_SLOTS)
-        rows = pl.ds(pl.multiple_of(i * W_ROWS, W_ROWS), W_ROWS)
-        return [pltpu.make_async_copy(ref.at[rows], buf.at[slot], wsem.at[j, slot]) for j, (ref, buf, _) in enumerate(weights)]
-
-    def cache_in(ref, buf, sem, g):
-        rows = pl.ds(g * per_group, per_group)
-        return pltpu.make_async_copy(ref.at[rows], buf.at[rows], sem.at[g])
+    blocks, _, blk = hid.shape
+    width = wbuf.shape[-1]
+    heads = width // head_dim
+    chips, core, chip, c_right, c_left, c_opp, partner, right, left = ring_place()
+    mine_k = core * chips + chip
 
     smalls = [pltpu.make_async_copy(src, dst, insem.at[j]) for j, (src, dst) in enumerate((
         (tok_in, tok_ref), (pos_in, pos_ref), (freq_in, freq_ref), (an_in, an_ref), (qn_in, qn_ref), (kn_in, kn_ref)))]
     for copy in smalls:
         copy.start()
-    for n in range(W_SLOTS):
-        for copy in w_copies(jnp.int32(n)):
+    bulk = []
+    for j, (ref, col) in enumerate(((wq_ref, mine_k), (wk_ref, core), (wv_ref, core))):
+        for i in range(blocks):
+            src = ref.at[pl.ds(i * blk, blk), pl.ds(pl.multiple_of(col * width, width), width)]
+            bulk.append(pltpu.make_async_copy(src, wbuf.at[j, i], wsem.at[j, i]))
+    pieces = csem.shape[1]
+    per = seqs // pieces
+    for g in range(pieces):
+        for j, (ref, buf) in enumerate(((kc_ref, kbuf), (vc_ref, vbuf))):
+            rows = pl.ds(g * per, per)
+            bulk.append(pltpu.make_async_copy(ref.at[rows], buf.at[rows], csem.at[j, g]))
+    issued = 0
+
+    def issue(count):
+        nonlocal issued
+        for copy in bulk[issued:issued + count]:
             copy.start()
+        issued += count
+
+    issue(6)
+    arrived = enter((partner, right, left))
     for copy in smalls:
         copy.wait()
 
     lanes = an_ref.shape[1]
-    total = jnp.zeros((seqs, 1), jnp.float32)
+    total = jnp.zeros((seqs, lanes), jnp.float32)
     for i in range(model // lanes):
         xf = tok_ref[:, i * lanes:(i + 1) * lanes].astype(jnp.float32)
-        total = total + jnp.sum(xf * xf, axis=-1, keepdims=True)
-    inv = lax.rsqrt(total / model + NORM_EPS)
-    per_step = W_ROWS // lanes
+        total = total + xf * xf
+    inv = lax.rsqrt(jnp.sum(total, axis=-1, keepdims=True) / model + NORM_EPS)
+    per_blk = blk // lanes
     for i in range(model // lanes):
         xf = tok_ref[:, i * lanes:(i + 1) * lanes].astype(jnp.float32)
         gain = an_ref[i:i + 1, :].astype(jnp.float32)
-        hid[i // per_step, :, (i % per_step) * lanes:(i % per_step + 1) * lanes] = (xf * inv * gain).astype(jnp.bfloat16)
+        hid[i // per_blk, :, (i % per_blk) * lanes:(i % per_blk + 1) * lanes] = (xf * inv * gain).astype(jnp.bfloat16)
 
     for b in range(seqs):
         cosb[b:b + 1, :] = jnp.full((1, head_dim), pos_ref[b], jnp.int32).astype(jnp.float32)
@@ -80,44 +111,128 @@
     sign = jnp.where(lax.broadcasted_iota(jnp.int32, angles.shape, 1) < head_dim // 2, -1.0, 1.0)
     sinb[...] = jnp.sin(angles) * sign
     cosb[...] = jnp.cos(angles)
-    for y in (yq, yk, yv):
-        y[...] = jnp.zeros_like(y)
-
-    def w_step(i, carry):
-        slot = lax.rem(i, W_SLOTS)
-        lhs = hid[i]
-        for copy, (_, buf, y) in zip(w_copies(i), weights):
-            copy.wait()
-            y[...] += jnp.dot(lhs, buf[slot], preferred_element_type=jnp.float32)
-
-        @pl.when(i + W_SLOTS < steps)
-        def _():
-            for copy in w_copies(i + W_SLOTS):
-                copy.start()
-
-        @pl.when(i + W_SLOTS >= steps)
-        def _():
-            g = i + W_SLOTS - steps
-            cache_in(kc_ref, kbuf, ksem, g).start()
-            cache_in(vc_ref, vbuf, vsem, g).start()
-
-        return carry
-
-    lax.fori_loop(0, steps, w_step, 0)
-    for g in range(W_SLOTS, groups):
-        cache_in(kc_ref, kbuf, ksem, g).start()
-        cache_in(vc_ref, vbuf, vsem, g).start()
-
     cos_full, sin_full = cosb[...], sinb[...]
+
+    def project(j, more):
+        y = None
+        for i in range(blocks):
+            bulk[j * blocks + i].wait()
+            issue(more)
+            part = jnp.dot(hid[i], wbuf[j, i], preferred_element_type=jnp.float32)
+            y = part if y is None else y + part
+        return [y[:, h * head_dim:(h + 1) * head_dim] for h in range(heads)]
+
+    def put(dst, base, values):
+        for h, value in enumerate(values):
+            dst[pl.ds(pl.multiple_of(base + h * seqs, seqs), seqs), :] = value
+
+    half_rows = heads // 2 * seqs
+
+    def q_half(k, h):
+        return qf.at[pl.ds(pl.multiple_of(k * heads * seqs + h * half_rows, half_rows), half_rows)]
+
+    q_gain = qn_ref[...].astype(jnp.float32)
+    put(qf, mine_k * heads * seqs, [norm_rope(p, q_gain, cos_full, sin_full) for p in project(0, 1)])
+    arrived()
+    count = 0
+    sent = []
+
+    def push(ref, peer):
+        nonlocal count
+        sent.append(send(ref, ref, ss.at[count], rs.at[count], peer))
+        count += 1
+        return sent[-1]
+
+    to_right_b = push(q_half(mine_k, 1), right)
+    to_left_a = push(q_half(mine_k, 0), left)
+    to_right_a = push(q_half(mine_k, 0), right)
+    to_left_b = push(q_half(mine_k, 1), left)
+    push(q_half(mine_k, 0), partner)
+    push(q_half(mine_k, 1), partner)
+
+    kv_rows = heads * seqs
+    kv_base = core * kv_rows
+    kv_part = pl.ds(pl.multiple_of(kv_base, kv_rows), kv_rows)
     k_gain = kn_ref[...].astype(jnp.float32)
-    q_gain = qn_ref[...].astype(jnp.float32)
-    for h in range(kv_heads):
-        cols = slice(h * head_dim, (h + 1) * head_dim)
-        rows = slice(h * seqs, (h + 1) * seqs)
-        kf[rows, :] = norm_rope(yk[:, cols], k_gain, cos_full, sin_full)
-        vf[rows, :] = yv[:, cols].astype(jnp.bfloat16).astype(jnp.float32)
-    for h in range(q_heads):
-        qf[h * seqs:(h + 1) * seqs, :] = norm_rope(yq[:, h * head_dim:(h + 1) * head_dim], q_gain, cos_full, sin_full)
+    put(kf, kv_base, [norm_rope(p, k_gain, cos_full, sin_full) for p in project(1, 2)])
+    push(kf.at[kv_part], partner)
+    put(vf, kv_base, [p.astype(jnp.bfloat16).astype(jnp.float32) for p in project(2, 3)])
+    push(vf.at[kv_part], partner)
+    issue(len(bulk) - issued)
+
+    k_left, k_right, k_opp = core * chips + c_left, core * chips + c_right, core * chips + c_opp
+    to_right_b.wait_recv()
+    fwd_right = push(q_half(k_left, 1), right)
+    to_left_a.wait_recv()
+    fwd_left = push(q_half(k_right, 0), left)
+    push(q_half(k_left, 1), partner)
+    push(q_half(k_right, 0), partner)
+    to_right_a.wait_recv()
+    push(q_half(k_left, 0), partner)
+    to_left_b.wait_recv()
+    push(q_half(k_right, 1), partner)
+    fwd_right.wait_recv()
+    push(q_half(k_opp, 1), partner)
+    fwd_left.wait_recv()
+    push(q_half(k_opp, 0), partner)
+    waited = (to_right_b, to_left_a, to_right_a, to_left_b, fwd_right, fwd_left)
+    for copy in sent:
+        if not any(copy is w for w in waited):
+            copy.wait_recv()
+        copy.wait_send()
+    for copy in bulk[3 * blocks:]:
+        copy.wait()
+
+
+def project_stage(tokens, positions, k_cache, v_cache, w_q, w_k, w_v, attn_norm, q_norm, k_norm, group):
+    seqs, model = tokens.shape
+    kv_heads, head_dim = k_cache.shape[2:]
+    q_heads = w_q.shape[1] // head_dim
+    width = w_q.shape[1] // group
+    blocks = 4
+    vmem = pl.BlockSpec(memory_space=pltpu.VMEM)
+    hbm = pl.BlockSpec(memory_space=pltpu.HBM)
+    dma = pltpu.SemaphoreType.DMA
+    return pl.pallas_call(
+        project_kernel,
+        name='project_stage',
+        out_shape=(
+            pltpu.VMEM((q_heads * seqs, head_dim), jnp.float32),
+            pltpu.VMEM((kv_heads * seqs, head_dim), jnp.float32),
+            pltpu.VMEM((kv_heads * seqs, head_dim), jnp.float32),
+            pltpu.VMEM(k_cache.shape, k_cache.dtype),
+            pltpu.VMEM(v_cache.shape, v_cache.dtype),
+        ),
+        in_specs=[hbm] * 11,
+        out_specs=(vmem,) * 5,
+        scratch_shapes=[
+            pltpu.SMEM(positions.shape, jnp.int32),
+            pltpu.VMEM(tokens.shape, tokens.dtype),
+            pltpu.VMEM((1, head_dim), jnp.float32),
+            pltpu.VMEM((model // 128, 128), attn_norm.dtype),
+            pltpu.VMEM((1, head_dim), q_norm.dtype),
+            pltpu.VMEM((1, head_dim), k_norm.dtype),
+            pltpu.VMEM((blocks, seqs, model // blocks), jnp.bfloat16),
+            pltpu.VMEM((3, blocks, model // blocks, width), jnp.bfloat16),
+            pltpu.VMEM((seqs, head_dim), jnp.float32),
+            pltpu.VMEM((seqs, head_dim), jnp.float32),
+            dma((6,)), dma((3, blocks)), dma((2, 8)), dma((16,)), dma((16,)),
+        ],
+        compiler_params=pltpu.CompilerParams(collective_id=1, has_side_effects=True, vmem_limit_bytes=24 * 1024 * 1024),
+    )(*in_hbm(positions, tokens, rope_frequencies(head_dim), attn_norm.reshape(-1, 128), q_norm[None, :], k_norm[None, :],
+              w_q, w_k, w_v, k_cache, v_cache))
+
+
+def attend_kernel(pos_in, qf, kf, vf, k_in, v_in, ko_ref, vo_ref, new_out, part_ref, kbuf, vbuf,
+                  pos_ref, new_ref, mstat, lstat, sbuf, ebuf, obuf, possem, newsem, kosem, vosem):
+    seqs, slots, kv_heads, head_dim = kbuf.shape
+    groups = kosem.shape[0]
+    per_group = seqs // groups
+    q_heads = qf.shape[0] // seqs
+    start = lax.axis_index('sp') * slots
+    pos_copy = pltpu.make_async_copy(pos_in, pos_ref, possem)
+    pos_copy.start()
+    pos_copy.wait()
 
     half = q_heads // 2
     cols = slots * kv_heads
@@ -133,8 +248,6 @@
     lstat[...] = jnp.zeros_like(lstat)
 
     def group_step(g, carry):
-        cache_in(kc_ref, kbuf, ksem, g).wait()
-        cache_in(vc_ref, vbuf, vsem, g).wait()
         m_acc, l_acc = mstat[...], lstat[...]
         members = [g * per_group + bb for bb in range(per_group)]
         for b in members:
@@ -192,67 +305,41 @@
         pltpu.make_async_copy(new_ref.at[rows], new_out.at[rows], newsem.at[g]).wait()
 
 
-def in_hbm(*arrays):
-    return [pltpu.with_memory_space_constraint(jnp.asarray(a), pltpu.HBM) for a in arrays]
-
-
-def local_stage(tokens, positions, k_cache, v_cache, w_q, w_k, w_v, attn_norm, q_norm, k_norm):
-    seqs, model = tokens.shape
-    slots, kv_heads, head_dim = k_cache.shape[1:]
-    q_heads = w_q.shape[1] // head_dim
+def attend_stage(positions, qf, kf, vf, k_vm, v_vm):
+    seqs, slots, kv_heads, head_dim = k_vm.shape
+    q_heads = qf.shape[0] // seqs
     groups = 8
     vmem = pl.BlockSpec(memory_space=pltpu.VMEM)
     anyspec = pl.BlockSpec(memory_space=pl.ANY)
     hbm = pl.BlockSpec(memory_space=pltpu.HBM)
-    part_shape = (q_heads // 2, 2 * seqs + STAT_ROWS, head_dim)
-    return pl.pallas_call(
-        local_kernel,
-        name='local_stage',
+    dma = pltpu.SemaphoreType.DMA
+    outs = pl.pallas_call(
+        attend_kernel,
+        name='attend_stage',
         out_shape=(
-            jax.ShapeDtypeStruct(k_cache.shape, k_cache.dtype),
-            jax.ShapeDtypeStruct(v_cache.shape, v_cache.dtype),
+            jax.ShapeDtypeStruct(k_vm.shape, k_vm.dtype),
+            jax.ShapeDtypeStruct(v_vm.shape, v_vm.dtype),
             jax.ShapeDtypeStruct((seqs, 2, kv_heads, head_dim), jnp.bfloat16),
-            pltpu.VMEM(part_shape, jnp.float32),
+            pltpu.VMEM((q_heads // 2, 2 * seqs + STAT_ROWS, head_dim), jnp.float32),
+            pltpu.VMEM(k_vm.shape, k_vm.dtype),
+            pltpu.VMEM(v_vm.shape, v_vm.dtype),
         ),
-        in_specs=[hbm] * 11,
-        out_specs=(anyspec, anyspec, anyspec, vmem),
+        in_specs=[hbm] + [vmem] * 5,
+        out_specs=(anyspec, anyspec, anyspec, vmem, vmem, vmem),
+        input_output_aliases={4: 4, 5: 5},
         scratch_shapes=[
             pltpu.SMEM(positions.shape, jnp.int32),
-            pltpu.VMEM(tokens.shape, tokens.dtype),
-            pltpu.VMEM((1, head_dim), jnp.float32),
-            pltpu.VMEM((model // 128, 128), attn_norm.dtype),
-            pltpu.VMEM((1, head_dim), q_norm.dtype),
-            pltpu.VMEM((1, head_dim), k_norm.dtype),
             pltpu.VMEM((seqs, 2, kv_heads, head_dim), jnp.bfloat16),
-            pltpu.SemaphoreType.DMA((6,)),
-            pltpu.SemaphoreType.DMA((groups,)),
-            pltpu.VMEM((model // W_ROWS, seqs, W_ROWS), jnp.bfloat16),
-            pltpu.VMEM((W_SLOTS, W_ROWS, w_q.shape[1]), jnp.bfloat16),
-            pltpu.VMEM((W_SLOTS, W_ROWS, w_k.shape[1]), jnp.bfloat16),
-            pltpu.VMEM((W_SLOTS, W_ROWS, w_v.shape[1]), jnp.bfloat16),
-            pltpu.VMEM((seqs, w_q.shape[1]), jnp.float32),
-            pltpu.VMEM((seqs, w_k.shape[1]), jnp.float32),
-            pltpu.VMEM((seqs, w_v.shape[1]), jnp.float32),
-            pltpu.VMEM((seqs, head_dim), jnp.float32),
-            pltpu.VMEM((seqs, head_dim), jnp.float32),
-            pltpu.VMEM(k_cache.shape, k_cache.dtype),
-            pltpu.VMEM(v_cache.shape, v_cache.dtype),
-            pltpu.VMEM((q_heads * seqs, head_dim), jnp.float32),
-            pltpu.VMEM((kv_heads * seqs, head_dim), jnp.float32),
-            pltpu.VMEM((kv_heads * seqs, head_dim), jnp.float32),
             pltpu.VMEM((q_heads, 128), jnp.float32),
             pltpu.VMEM((q_heads, 128), jnp.float32),
             pltpu.VMEM((seqs // groups, q_heads, slots * kv_heads), jnp.float32),
             pltpu.VMEM((seqs // groups, q_heads, slots * kv_heads), jnp.bfloat16),
             pltpu.VMEM((seqs // groups, q_heads, head_dim), jnp.float32),
-            pltpu.SemaphoreType.DMA((3, W_SLOTS)),
-            pltpu.SemaphoreType.DMA((groups,)),
-            pltpu.SemaphoreType.DMA((groups,)),
-            pltpu.SemaphoreType.DMA((groups,)),
-            pltpu.SemaphoreType.DMA((groups,)),
+            dma, dma((groups,)), dma((groups,)), dma((groups,)),
         ],
-        compiler_params=pltpu.CompilerParams(vmem_limit_bytes=46 * 1024 * 1024),
-    )(*in_hbm(positions, tokens, rope_frequencies(head_dim), attn_norm.reshape(-1, 128), q_norm[None, :], k_norm[None, :]), w_q, w_k, w_v, k_cache, v_cache)
+        compiler_params=pltpu.CompilerParams(vmem_limit_bytes=16 * 1024 * 1024),
+    )(*in_hbm(positions), qf, kf, vf, k_vm, v_vm)
+    return outs[:4]
 
 
 def combine(pieces, seqs, rows_out, final=False):
@@ -298,12 +385,6 @@
     for peer in (partner, right, left):
         pl.semaphore_signal(barrier, inc=1, device_id={'sp': peer}, device_id_type=MESH)
     pl.semaphore_wait(barrier, 3)
-
-    def send(src, dst, ss, rs, peer):
-        copy = pltpu.make_async_remote_copy(src_ref=src, dst_ref=dst, send_sem=ss, recv_sem=rs,
-                                            device_id={'sp': peer}, device_id_type=MESH)
-        copy.start()
-        return copy
 
     order = (c_opp, c_right, c_left, chip)
     halves = 2 * chips
@@ -449,7 +530,8 @@
     group = mesh.shape['sp']
 
     def device_step(tokens, positions, k_cache, v_cache, w_q, w_k, w_v, w_o, attn_norm, q_norm, k_norm):
-        k_upd, v_upd, new_kv, part = local_stage(tokens, positions, k_cache, v_cache, w_q, w_k, w_v, attn_norm, q_norm, k_norm)
+        shared = project_stage(tokens, positions, k_cache, v_cache, w_q, w_k, w_v, attn_norm, q_norm, k_norm, group)
+        k_upd, v_upd, new_kv, part = attend_stage(positions, *shared)
         block_out = tail_stage(part, w_o, tokens, group)
         return block_out, k_upd, v_upd, new_kv
 

time: 56.8 us -> 49.6 us (0.87)
  Pallas kernels: 55.3 us -> 48.1 us
    pallas_call x1 -> x2, Pallas kernels: 30.3 us -> 24.6 us  [the longest x1 16.2 us: project_stage(): pl.pallas_call(project_kernel, name='project_stage', out_shape=(pltpu.VME...]
    pallas_call x1, Pallas kernels: 25 us -> 23.5 us  [tail_stage(): pl.pallas_call(tail_kernel, name='tail_stage', out_shape=pltpu.VMEM((seqs...]
where the time goes in v4:
time: 49.6 us; the launch traced here: 49.5 us
  Pallas kernels  48.1 us (97%)
  local copies, waits for them, and re-layouts  0.8 us (2%)
  between operations  0.66 us (1%)
    pallas_call x1, Pallas kernels, tail_stage(): pl.pallas_call(tail_kernel, name='tail_stage', out_shape=pltpu.VMEM((seqs...  23.5 us
    pallas_call x1, Pallas kernels, project_stage(): pl.pallas_call(project_kernel, name='project_stage', out_shape=(pltpu.VME...  16.2 us
    pallas_call x1, Pallas kernels, attend_stage(): pl.pallas_call(attend_kernel, name='attend_stage', out_shape=(jax.ShapeDt...  8.44 us

profile of v4, /device:TPU:113, one launch (start us, length us, event | category | flops | bytes accessed | tf_op | source)
XLA Modules:
  0.0 49.5 jit_solution(2852715680612360757)
XLA Ops:
  0.6 16.2 %project_stage.1 = (f32[2048,128]{1,0:T(8,128)S(1)}, f32[512,128]{1,0:T(8,128)S(1)}, f32[512,128]{1,0:T(8,128)S(1)}, bf16[64,64,8,128]{3,2,1,0:T(8,128)(2,1)S(1)}, bf16[64,64,8,128]{3,2,1,0:T(8,128)(2,1)S(1)}) custom-call(s32[64]{0:T(128)} %pos_in.3, bf16[64,4096]{1,0:T(8,128)(2,1)} %tok_in.3, f32[1,128]{1,0:T(1,128)} %constant.2.clone.freq_in, ...), custom_call_target="tpu_custom_call" | custom-call | tf_op jit(solution)/shard_map/project_stage/pallas_call | solution.py:196
  16.8 8.4 %attend_stage.1 = (bf16[64,64,8,128]{3,2,1,0:T(8,128)(2,1)}, bf16[64,64,8,128]{3,2,1,0:T(8,128)(2,1)}, bf16[64,2,8,128]{3,2,1,0:T(8,128)(2,1)}, f32[16,136,128]{...) custom-call(s32[64]{0:T(128)} %pos_in.3, ...), custom_call_target="tpu_custom_call", output_to_operand_aliasing={{4}: (4, {}), {5}: (5, {})} | custom-call | tf_op jit(solution)/shard_map/attend_stage/pallas_call | solution.py:316
  25.3 23.5 %tail_stage.1 = bf16[64,4096]{1,0:T(8,128)(2,1)S(1)} custom-call(f32[16,136,128]{2,1,0:T(8,128)S(1)} %get-tuple-element.18.mine, bf16[4096,4096]{1,0:T(8,128)(2,1)} %wo_ref.1, bf16[64,4096]{1,0:T(8,128)(2,1)} %tok_in.3), custom_call_target="tpu_custom_call" | custom-call | tf_op jit(solution)/shard_map/tail_stage/pallas_call | solution.py:505
  48.7 0.8 %copy.21 = bf16[64,4096]{1,0:T(8,128)(2,1)} copy(bf16[64,4096]{1,0:T(8,128)(2,1)S(1)} %tail_stage.1) | data formatting | bytes 1048576

commit v5 on v4

v5 whole, which is shorter than its diff:
```python
import functools

import jax
import jax.numpy as jnp
import numpy as np
from jax import lax
from jax.experimental import pallas as pl
from jax.experimental.pallas import tpu as pltpu
from jax.sharding import PartitionSpec as P

NORM_EPS = 1e-6
ROPE_THETA = 1000000.0
NEG_FILL = -1e30
MESH = pl.DeviceIdType.MESH
STAT_ROWS = 8


def in_hbm(*arrays):
    return [pltpu.with_memory_space_constraint(jnp.asarray(a), pltpu.HBM) for a in arrays]


def rope_frequencies(head_dim):
    inv_freq = ROPE_THETA ** (-np.arange(head_dim // 2, dtype=np.float64) * 2.0 / head_dim)
    return np.concatenate([inv_freq, inv_freq])[None, :].astype(np.float32)


def norm_rope(proj, gain, cos_full, sin_full):
    values = proj.astype(jnp.bfloat16).astype(jnp.float32)
    scale = lax.rsqrt(jnp.mean(values * values, axis=-1, keepdims=True) + NORM_EPS)
    normed = values * scale * gain
    turned = pltpu.roll(normed, normed.shape[-1] // 2, 1)
    return (normed * cos_full + turned * sin_full).astype(jnp.bfloat16).astype(jnp.float32)


def ring_place():
    me = lax.axis_index('sp')
    chips = lax.axis_size('sp') // 2
    core, chip = lax.rem(me, 2), me // 2
    c_right, c_left, c_opp = lax.rem(chip + 1, chips), lax.rem(chip + chips - 1, chips), lax.rem(chip + 2, chips)
    return chips, core, chip, c_right, c_left, c_opp, chip * 2 + 1 - core, c_right * 2 + core, c_left * 2 + core


def enter(peers):
    barrier = pltpu.get_barrier_semaphore()
    for peer in peers:
        pl.semaphore_signal(barrier, inc=1, device_id={'sp': peer}, device_id_type=MESH)
    return lambda: pl.semaphore_wait(barrier, len(peers))


def send(src, dst, ss, rs, peer):
    copy = pltpu.make_async_remote_copy(src_ref=src, dst_ref=dst, send_sem=ss, recv_sem=rs,
                                        device_id={'sp': peer}, device_id_type=MESH)
    copy.start()
    return copy


def project_kernel(pos_in, tok_in, freq_in, an_in, qn_in, kn_in, wq_ref, wk_ref, wv_ref, kc_ref, vc_ref,
                   qf, kf, vf, kbuf, vbuf,
                   pos_ref, tok_ref, freq_ref, an_ref, qn_ref, kn_ref, hid, wbuf, cosb, sinb, insem, wsem, csem, ss, rs):
    seqs, model = tok_ref.shape
    head_dim = qn_ref.shape[-1]
    blocks, _, blk = hid.shape
    width = wbuf.shape[-1]
    heads = width // head_dim
    chips, core, chip, c_right, c_left, c_opp, partner, right, left = ring_place()
    mine_k = core * chips + chip

    smalls = [pltpu.make_async_copy(src, dst, insem.at[j]) for j, (src, dst) in enumerate((
        (tok_in, tok_ref), (pos_in, pos_ref), (freq_in, freq_ref), (an_in, an_ref), (qn_in, qn_ref), (kn_in, kn_ref)))]
    for copy in smalls:
        copy.start()
    bulk = []
    k_left, k_right, k_opp = core * chips + c_left, core * chips + c_right, core * chips + c_opp
    for j, (ref, col) in enumerate(((wq_ref, mine_k), (wq_ref, k_opp), (wk_ref, core), (wv_ref, core))):
        for i in range(blocks):
            src = ref.at[pl.ds(i * blk, blk), pl.ds(pl.multiple_of(col * width, width), width)]
            bulk.append(pltpu.make_async_copy(src, wbuf.at[j, i], wsem.at[j, i]))
    pieces = csem.shape[1]
    per = seqs // pieces
    for g in range(pieces):
        for j, (ref, buf) in enumerate(((kc_ref, kbuf), (vc_ref, vbuf))):
            rows = pl.ds(g * per, per)
            bulk.append(pltpu.make_async_copy(ref.at[rows], buf.at[rows], csem.at[j, g]))
    issued = 0

    def issue(count):
        nonlocal issued
        for copy in bulk[issued:issued + count]:
            copy.start()
        issued += count

    issue(7)
    arrived = enter((partner, right, left))
    for copy in smalls:
        copy.wait()

    lanes = an_ref.shape[1]
    total = jnp.zeros((seqs, lanes), jnp.float32)
    for i in range(model // lanes):
        xf = tok_ref[:, i * lanes:(i + 1) * lanes].astype(jnp.float32)
        total = total + xf * xf
    inv = lax.rsqrt(jnp.sum(total, axis=-1, keepdims=True) / model + NORM_EPS)
    per_blk = blk // lanes
    for i in range(model // lanes):
        xf = tok_ref[:, i * lanes:(i + 1) * lanes].astype(jnp.float32)
        gain = an_ref[i:i + 1, :].astype(jnp.float32)
        hid[i // per_blk, :, (i % per_blk) * lanes:(i % per_blk + 1) * lanes] = (xf * inv * gain).astype(jnp.bfloat16)

    for b in range(seqs):
        cosb[b:b + 1, :] = jnp.full((1, head_dim), pos_ref[b], jnp.int32).astype(jnp.float32)
    angles = cosb[...] * freq_ref[...]
    sign = jnp.where(lax.broadcasted_iota(jnp.int32, angles.shape, 1) < head_dim // 2, -1.0, 1.0)
    sinb[...] = jnp.sin(angles) * sign
    cosb[...] = jnp.cos(angles)
    cos_full, sin_full = cosb[...], sinb[...]

    def project(j, more):
        y = None
        for i in range(blocks):
            bulk[j * blocks + i].wait()
            issue(more)
            part = jnp.dot(hid[i], wbuf[j, i], preferred_element_type=jnp.float32)
            y = part if y is None else y + part
        return [y[:, h * head_dim:(h + 1) * head_dim] for h in range(heads)]

    def put(dst, base, values):
        for h, value in enumerate(values):
            dst[pl.ds(pl.multiple_of(base + h * seqs, seqs), seqs), :] = value

    half_rows = heads // 2 * seqs

    def q_half(k, h):
        return qf.at[pl.ds(pl.multiple_of(k * heads * seqs + h * half_rows, half_rows), half_rows)]

    q_gain = qn_ref[...].astype(jnp.float32)
    put(qf, mine_k * heads * seqs, [norm_rope(p, q_gain, cos_full, sin_full) for p in project(0, 1)])
    arrived()
    count = 0
    sent = []

    def push(ref, peer):
        nonlocal count
        sent.append(send(ref, ref, ss.at[count], rs.at[count], peer))
        count += 1
        return sent[-1]

    own = [[push(q_half(mine_k, h), peer) for peer in (right, left)] for h in range(2)]
    push(q_half(mine_k, 0), partner)
    push(q_half(mine_k, 1), partner)
    put(qf, k_opp * heads * seqs, [norm_rope(p, q_gain, cos_full, sin_full) for p in project(1, 2)])
    push(q_half(k_opp, 0), partner)
    push(q_half(k_opp, 1), partner)

    kv_rows = heads * seqs
    kv_base = core * kv_rows
    kv_part = pl.ds(pl.multiple_of(kv_base, kv_rows), kv_rows)
    k_gain = kn_ref[...].astype(jnp.float32)
    put(kf, kv_base, [norm_rope(p, k_gain, cos_full, sin_full) for p in project(2, 2)])
    push(kf.at[kv_part], partner)
    put(vf, kv_base, [p.astype(jnp.bfloat16).astype(jnp.float32) for p in project(3, 2)])
    push(vf.at[kv_part], partner)
    issue(len(bulk) - issued)

    for h in range(2):
        for from_peer, k in zip(own[h], (k_left, k_right)):
            from_peer.wait_recv()
            push(q_half(k, h), partner)
    waited = own[0] + own[1]
    for copy in sent:
        if not any(copy is w for w in waited):
            copy.wait_recv()
        copy.wait_send()
    for copy in bulk[4 * blocks:]:
        copy.wait()


def project_stage(tokens, positions, k_cache, v_cache, w_q, w_k, w_v, attn_norm, q_norm, k_norm, group):
    seqs, model = tokens.shape
    kv_heads, head_dim = k_cache.shape[2:]
    q_heads = w_q.shape[1] // head_dim
    width = w_q.shape[1] // group
    blocks = 4
    vmem = pl.BlockSpec(memory_space=pltpu.VMEM)
    hbm = pl.BlockSpec(memory_space=pltpu.HBM)
    dma = pltpu.SemaphoreType.DMA
    return pl.pallas_call(
        project_kernel,
        name='project_stage',
        out_shape=(
            pltpu.VMEM((q_heads * seqs, head_dim), jnp.float32),
            pltpu.VMEM((kv_heads * seqs, head_dim), jnp.float32),
            pltpu.VMEM((kv_heads * seqs, head_dim), jnp.float32),
            pltpu.VMEM(k_cache.shape, k_cache.dtype),
            pltpu.VMEM(v_cache.shape, v_cache.dtype),
        ),
        in_specs=[hbm] * 11,
        out_specs=(vmem,) * 5,
        scratch_shapes=[
            pltpu.SMEM(positions.shape, jnp.int32),
            pltpu.VMEM(tokens.shape, tokens.dtype),
            pltpu.VMEM((1, head_dim), jnp.float32),
            pltpu.VMEM((model // 128, 128), attn_norm.dtype),
            pltpu.VMEM((1, head_dim), q_norm.dtype),
            pltpu.VMEM((1, head_dim), k_norm.dtype),
            pltpu.VMEM((blocks, seqs, model // blocks), jnp.bfloat16),
            pltpu.VMEM((4, blocks, model // blocks, width), jnp.bfloat16),
            pltpu.VMEM((seqs, head_dim), jnp.float32),
            pltpu.VMEM((seqs, head_dim), jnp.float32),
            dma((6,)), dma((4, blocks)), dma((2, 8)), dma((16,)), dma((16,)),
        ],
        compiler_params=pltpu.CompilerParams(collective_id=1, has_side_effects=True, vmem_limit_bytes=24 * 1024 * 1024),
    )(*in_hbm(positions, tokens, rope_frequencies(head_dim), attn_norm.reshape(-1, 128), q_norm[None, :], k_norm[None, :],
              w_q, w_k, w_v, k_cache, v_cache))


def attend_kernel(pos_in, qf, kf, vf, k_in, v_in, ko_ref, vo_ref, new_out, part_ref, kbuf, vbuf,
                  pos_ref, new_ref, mstat, lstat, sbuf, ebuf, obuf, possem, newsem, kosem, vosem):
    seqs, slots, kv_heads, head_dim = kbuf.shape
    groups = kosem.shape[0]
    per_group = seqs // groups
    q_heads = qf.shape[0] // seqs
    start = lax.axis_index('sp') * slots
    pos_copy = pltpu.make_async_copy(pos_in, pos_ref, possem)
    pos_copy.start()
    pos_copy.wait()

    def write_step(g, carry):
        for bb in range(per_group):
            b = g * per_group + bb
            local = pos_ref[b] - start
            here = (local >= 0) & (local < slots)
            at = jnp.clip(local, 0, slots - 1)
            k_new = kf[pl.ds(b, kv_heads, stride=seqs), :]
            v_new = vf[pl.ds(b, kv_heads, stride=seqs), :]
            new_ref[b, 0] = k_new.astype(jnp.bfloat16)
            new_ref[b, 1] = v_new.astype(jnp.bfloat16)
            kbuf[b, at] = jnp.where(here, k_new, kbuf[b, at].astype(jnp.float32)).astype(jnp.bfloat16)
            vbuf[b, at] = jnp.where(here, v_new, vbuf[b, at].astype(jnp.float32)).astype(jnp.bfloat16)
        for copy in writes(g):
            copy.start()
        return carry

    def writes(g):
        rows = pl.ds(g * per_group, per_group)
        return (pltpu.make_async_copy(kbuf.at[rows], ko_ref.at[rows], kosem.at[g]),
                pltpu.make_async_copy(vbuf.at[rows], vo_ref.at[rows], vosem.at[g]),
                pltpu.make_async_copy(new_ref.at[rows], new_out.at[rows], newsem.at[g]))

    lax.fori_loop(0, groups, write_step, 0)

    cols = slots * kv_heads
    row_id = lax.broadcasted_iota(jnp.int32, (q_heads, cols), 0)
    col_id = lax.broadcasted_iota(jnp.int32, (q_heads, cols), 1)
    head_ok = row_id // (q_heads // kv_heads) == col_id % kv_heads
    slot_key = jnp.where(head_ok, col_id // kv_heads, slots * 1024)
    lane = lax.broadcasted_iota(jnp.int32, (q_heads, 128), 1)
    score_scale = head_dim ** -0.5
    mstat[...] = jnp.zeros_like(mstat)
    lstat[...] = jnp.zeros_like(lstat)

    def group_step(g, carry):
        m_acc, l_acc = mstat[...], lstat[...]
        members = [g * per_group + bb for bb in range(per_group)]
        for bb, b in enumerate(members):
            q_b = qf[pl.ds(b, q_heads, stride=seqs), :].astype(jnp.bfloat16)
            k_b = kbuf[b].reshape(cols, head_dim)
            sbuf[bb] = lax.dot_general(q_b, k_b, (((1,), (1,)), ((), ())), preferred_element_type=jnp.float32)
        for bb, b in enumerate(members):
            live = slot_key <= pos_ref[b] - start
            s = jnp.where(live, sbuf[bb] * score_scale, NEG_FILL)
            m = jnp.max(s, axis=-1, keepdims=True)
            e = jnp.where(live, jnp.exp(s - m), 0.0)
            l = jnp.sum(e, axis=-1, keepdims=True)
            ebuf[bb] = e.astype(jnp.bfloat16)
            m_acc = jnp.where(lane == b, m, m_acc)
            l_acc = jnp.where(lane == b, l, l_acc)
        for bb, b in enumerate(members):
            obuf[bb] = jnp.dot(ebuf[bb], vbuf[b].reshape(cols, head_dim), preferred_element_type=jnp.float32)
        for bb, b in enumerate(members):
            for h in range(q_heads):
                part_ref[h, pl.ds(b, 1), :] = obuf[bb, h:h + 1, :]
        mstat[...] = m_acc
        lstat[...] = l_acc
        return carry

    lax.fori_loop(0, groups, group_step, 0)

    for h in range(q_heads):
        part_ref[h, seqs:seqs + 1, :] = mstat[h:h + 1, :]
        part_ref[h, seqs + 1:seqs + 2, :] = lstat[h:h + 1, :]
        part_ref[h, seqs + 2:seqs + STAT_ROWS, :] = jnp.zeros((STAT_ROWS - 2, 128), jnp.float32)
    for g in range(groups):
        for copy in writes(g):
            copy.wait()


def attend_stage(positions, qf, kf, vf, k_vm, v_vm):
    seqs, slots, kv_heads, head_dim = k_vm.shape
    q_heads = qf.shape[0] // seqs
    groups = 8
    vmem = pl.BlockSpec(memory_space=pltpu.VMEM)
    anyspec = pl.BlockSpec(memory_space=pl.ANY)
    hbm = pl.BlockSpec(memory_space=pltpu.HBM)
    dma = pltpu.SemaphoreType.DMA
    outs = pl.pallas_call(
        attend_kernel,
        name='attend_stage',
        out_shape=(
            jax.ShapeDtypeStruct(k_vm.shape, k_vm.dtype),
            jax.ShapeDtypeStruct(v_vm.shape, v_vm.dtype),
            jax.ShapeDtypeStruct((seqs, 2, kv_heads, head_dim), jnp.bfloat16),
            pltpu.VMEM((q_heads, seqs + STAT_ROWS, head_dim), jnp.float32),
            pltpu.VMEM(k_vm.shape, k_vm.dtype),
            pltpu.VMEM(v_vm.shape, v_vm.dtype),
        ),
        in_specs=[hbm] + [vmem] * 5,
        out_specs=(anyspec, anyspec, anyspec, vmem, vmem, vmem),
        input_output_aliases={4: 4, 5: 5},
        scratch_shapes=[
            pltpu.SMEM(positions.shape, jnp.int32),
            pltpu.VMEM((seqs, 2, kv_heads, head_dim), jnp.bfloat16),
            pltpu.VMEM((q_heads, 128), jnp.float32),
            pltpu.VMEM((q_heads, 128), jnp.float32),
            pltpu.VMEM((seqs // groups, q_heads, slots * kv_heads), jnp.float32),
            pltpu.VMEM((seqs // groups, q_heads, slots * kv_heads), jnp.bfloat16),
            pltpu.VMEM((seqs // groups, q_heads, head_dim), jnp.float32),
            dma, dma((groups,)), dma((groups,)), dma((groups,)),
        ],
        compiler_params=pltpu.CompilerParams(vmem_limit_bytes=16 * 1024 * 1024),
    )(*in_hbm(positions), qf, kf, vf, k_vm, v_vm)
    return outs[:4]


def merge(pieces, seqs, final=False):
    stats = [jnp.transpose(ref[seqs:seqs + STAT_ROWS, :], (1, 0))[:seqs] for ref in pieces]
    peak = functools.reduce(jnp.maximum, [t[:, 0:1] for t in stats])
    factors = [jnp.exp(t[:, 0:1] - peak) for t in stats]
    total = functools.reduce(jnp.add, [f * t[:, 1:2] for f, t in zip(factors, stats)])
    rows = functools.reduce(jnp.add, [f * ref[0:seqs, :] for f, ref in zip(factors, pieces)])
    if final:
        return rows / total
    both = jnp.concatenate([peak, total, jnp.zeros((seqs, STAT_ROWS - 2), jnp.float32)], axis=1)
    both = jnp.concatenate([both, jnp.zeros((128 - seqs, STAT_ROWS), jnp.float32)], axis=0)
    return rows, jnp.transpose(both, (1, 0))


def tail_kernel(mine, wo_ref, tok_in, out_ref, tok_ref, toksem, pin, away, kept, in1, out2, in2, att, wov, res,
                wsem, s0, r0, s1, r1, s2, r2, s3, r3, s4, r4, s5, r5):
    seqs, model = tok_ref.shape
    per = away.shape[1]
    tok_copy = pltpu.make_async_copy(tok_in, tok_ref, toksem)
    tok_copy.start()
    chips, core, chip, _, _, _, partner, _, _ = ring_place()
    near, far = chip + 1 - 2 * lax.rem(chip, 2), chips - 1 - chip
    first = (near * 2 + core, far * 2 + core)
    second = (first[1], first[0])
    sel = (lax.rem((chip + 1) // 2, 2), chip // 2)
    keep = [2 * c + sel[c] for c in range(2)]
    give = [2 * c + 1 - sel[c] for c in range(2)]
    arrived = enter((partner, first[0], first[1]))
    k_rows = wov.shape[1]

    def wo_copy(k):
        return pltpu.make_async_copy(wo_ref.at[pl.ds(pl.multiple_of(k * k_rows, k_rows), k_rows)], wov.at[k], wsem.at[k])

    arrived()
    sent = []

    def push(src, dst, ss, rs, peer):
        sent.append(send(src, dst, ss, rs, peer))
        return sent[-1]

    order = give + keep
    heads = per * 4
    pair = [push(mine.at[pl.ds((1 - core) * heads + q * per, per)], pin.at[i], s0.at[i], r0.at[i], partner)
            for i, q in enumerate(order)]
    for k in range(2):
        wo_copy(k).start()

    def put(dst, merged):
        rows, stat = merged
        dst[0:seqs, :] = rows
        dst[seqs:seqs + STAT_ROWS, :] = stat

    pair[0].wait_recv()
    pair[1].wait_recv()
    step1 = [[], []]
    for i in range(per):
        for c in range(2):
            put(away.at[c, i], merge([mine.at[core * heads + give[c] * per + i], pin.at[c, i]], seqs))
        for c in range(2):
            step1[c].append(push(away.at[c, i], in1.at[c, i], s1.at[c, i], r1.at[c, i], first[c]))
    for k in range(2, 8):
        wo_copy(k).start()
    pair[2].wait_recv()
    pair[3].wait_recv()
    for i in range(per):
        for c in range(2):
            put(kept.at[c, i], merge([mine.at[core * heads + keep[c] * per + i], pin.at[2 + c, i]], seqs))
    step2 = [[], []]
    for i in range(per):
        for c in range(2):
            step1[c][i].wait_recv()
        for c in range(2):
            put(out2.at[c, i], merge([kept.at[c, i], in1.at[c, i]], seqs))
        for c in range(2):
            step2[c].append(push(out2.at[c, i], in2.at[c, i], s2.at[c, i], r2.at[c, i], second[c]))
    step3, own = [[], []], [[], []]
    blocks = [core * 4 + keep[c] for c in range(2)]

    def rows_of(k, i):
        return att.at[k, pl.ds(i * seqs, seqs)]

    for i in range(per):
        for c in range(2):
            step2[c][i].wait_recv()
        for c in range(2):
            done = merge([out2.at[c, i], in2.at[c, i]], seqs, final=True)
            att[blocks[c], i * seqs:(i + 1) * seqs, :] = done.astype(jnp.bfloat16).astype(jnp.float32)
        for c in range(2):
            piece = rows_of(blocks[c], i)
            step3[c].append(push(piece, piece, s3.at[c, i], r3.at[c, i], first[c]))
            own[c].append(push(piece, piece, s4.at[c, i], r4.at[c, i], partner))

    cols = 512

    def multiply(k, fresh=False):
        wo_copy(k).wait()
        lhs = jnp.concatenate([att[k, i * seqs:(i + 1) * seqs, :] for i in range(per)], axis=1).astype(jnp.bfloat16)
        for i in range(model // cols):
            off = slice(i * cols, (i + 1) * cols)
            y = jnp.dot(lhs, wov[k, :, off], preferred_element_type=jnp.float32)
            res[:, off] = y if fresh else res[:, off] + y

    other = (1 - core) * 4
    multiply(blocks[0], fresh=True)
    multiply(blocks[1])
    for c in range(2):
        for i in range(per):
            own[c][i].wait_recv()
        multiply(other + keep[c])
    passed = [[], []]
    for i in range(per):
        for c in range(2):
            step3[c][i].wait_recv()
            piece = rows_of(core * 4 + give[c], i)
            passed[c].append(push(piece, piece, s5.at[c, i], r5.at[c, i], partner))
    for c in range(2):
        multiply(core * 4 + give[c])
    for c in range(2):
        for i in range(per):
            passed[c][i].wait_recv()
        multiply(other + give[c])
    tok_copy.wait()
    out_ref[...] = (tok_ref[...].astype(jnp.float32) + res[...]).astype(jnp.bfloat16)
    for copy in sent:
        copy.wait_send()


def tail_stage(part, w_o, tokens, group):
    seqs, model = tokens.shape
    q_heads, rows, head_dim = part.shape
    per = q_heads // group
    vmem = pl.BlockSpec(memory_space=pltpu.VMEM)
    hbm = pl.BlockSpec(memory_space=pltpu.HBM)
    dma = pltpu.SemaphoreType.DMA
    sums = pltpu.VMEM((2, per, rows, head_dim), jnp.float32)
    return pl.pallas_call(
        tail_kernel,
        name='tail_stage',
        out_shape=pltpu.VMEM((seqs, model), jnp.bfloat16),
        in_specs=[vmem, hbm, hbm],
        out_specs=vmem,
        scratch_shapes=[
            pltpu.VMEM((seqs, model), tokens.dtype),
            dma,
            pltpu.VMEM((4, per, rows, head_dim), jnp.float32),
            sums, sums, sums, sums, sums,
            pltpu.VMEM((group, per * seqs, head_dim), jnp.float32),
            pltpu.VMEM((group, w_o.shape[0] // group, model), jnp.bfloat16),
            pltpu.VMEM((seqs, model), jnp.float32),
            dma((group,)), dma((4,)), dma((4,)),
        ] + [dma((2, per))] * 10,
        compiler_params=pltpu.CompilerParams(collective_id=0, has_side_effects=True, vmem_limit_bytes=44 * 1024 * 1024),
    )(part, *in_hbm(w_o, tokens))


def solution(mesh):
    cache_spec = P('dp', 'sp', None, None)
    group = mesh.shape['sp']

    def device_step(tokens, positions, k_cache, v_cache, w_q, w_k, w_v, w_o, attn_norm, q_norm, k_norm):
        shared = project_stage(tokens, positions, k_cache, v_cache, w_q, w_k, w_v, attn_norm, q_norm, k_norm, group)
        k_upd, v_upd, new_kv, part = attend_stage(positions, *shared)
        block_out = tail_stage(part, w_o, tokens, group)
        return block_out, k_upd, v_upd, new_kv

    return jax.shard_map(device_step, mesh=mesh, in_specs=(P('dp', None), P('dp'), cache_spec, cache_spec, P(), P(), P(), P(), P(), P(), P()), out_specs=(P('dp', None), cache_spec, cache_spec, P('dp', None, None, None)), check_vma=False)
```

time: 49.6 us -> 45 us (0.907)
  Pallas kernels: 48.1 us -> 43.5 us
    pallas_call x1, Pallas kernels: 23.5 us -> 21.5 us  [tail_stage(): pl.pallas_call(tail_kernel, name='tail_stage', out_shape=pltpu.VMEM((seqs...]
    pallas_call x1, Pallas kernels: 16.2 us -> 14.3 us  [project_stage(): pl.pallas_call(project_kernel, name='project_stage', out_shape=(pltpu.VME...]
    pallas_call x1, Pallas kernels: 8.44 us -> 7.68 us  [attend_stage(): pl.pallas_call(attend_kernel, name='attend_stage', out_shape=(jax.ShapeDt...]
where the time goes in v5:
time: 45 us; the launch traced here: 44.9 us
  Pallas kernels  43.5 us (97%)
  local copies, waits for them, and re-layouts  0.8 us (2%)
  between operations  0.66 us (1%)
    pallas_call x1, Pallas kernels, tail_stage(): pl.pallas_call(tail_kernel, name='tail_stage', out_shape=pltpu.VMEM((seqs...  21.5 us
    pallas_call x1, Pallas kernels, project_stage(): pl.pallas_call(project_kernel, name='project_stage', out_shape=(pltpu.VME...  14.3 us
    pallas_call x1, Pallas kernels, attend_stage(): pl.pallas_call(attend_kernel, name='attend_stage', out_shape=(jax.ShapeDt...  7.68 us

profile of v5, /device:TPU:113, one launch (start us, length us, event | category | flops | bytes accessed | tf_op | source)
XLA Modules:
  0.0 44.9 jit_solution(13301856572997040975)
XLA Ops:
  0.6 14.3 %project_stage.1 = (f32[2048,128]{1,0:T(8,128)S(1)}, f32[512,128]{1,0:T(8,128)S(1)}, f32[512,128]{1,0:T(8,128)S(1)}, bf16[64,64,8,128]{3,2,1,0:T(8,128)(2,1)S(1)}, bf16[64,64,8,128]{3,2,1,0:T(8,128)(2,1)S(1)}) custom-call(s32[64]{0:T(128)} %pos_in.3, bf16[64,4096]{1,0:T(8,128)(2,1)} %tok_in.3, f32[1,128]{1,0:T(1,128)} %constant.2.clone.freq_in, ...), custom_call_target="tpu_custom_call" | custom-call | tf_op jit(solution)/shard_map/project_stage/pallas_call | solution.py:186
  14.9 7.7 %attend_stage.1 = (bf16[64,64,8,128]{3,2,1,0:T(8,128)(2,1)}, bf16[64,64,8,128]{3,2,1,0:T(8,128)(2,1)}, bf16[64,2,8,128]{3,2,1,0:T(8,128)(2,1)}, f32[32,72,128]{2...) custom-call(s32[64]{0:T(128)} %pos_in.3, ...), custom_call_target="tpu_custom_call", output_to_operand_aliasing={{4}: (4, {}), {5}: (5, {})} | custom-call | tf_op jit(solution)/shard_map/attend_stage/pallas_call | solution.py:305
  22.6 21.5 %tail_stage.1 = bf16[64,4096]{1,0:T(8,128)(2,1)S(1)} custom-call(f32[32,72,128]{2,1,0:T(8,128)S(1)} %get-tuple-element.18.mine, bf16[4096,4096]{1,0:T(8,128)(2,1)} %wo_ref.1, bf16[64,4096]{1,0:T(8,128)(2,1)} %tok_in.3), custom_call_target="tpu_custom_call" | custom-call | tf_op jit(solution)/shard_map/tail_stage/pallas_call | solution.py:468
  44.2 0.8 %copy.21 = bf16[64,4096]{1,0:T(8,128)(2,1)} copy(bf16[64,4096]{1,0:T(8,128)(2,1)S(1)} %tail_stage.1) | data formatting | bytes 1048576

commit v6 on v5

--- a/solution.py
+++ b/solution.py
@@ -89,7 +89,7 @@
             copy.start()
         issued += count
 
-    issue(7)
+    issue(8)
     arrived = enter((partner, right, left))
     for copy in smalls:
         copy.wait()
@@ -133,7 +133,7 @@
         return qf.at[pl.ds(pl.multiple_of(k * heads * seqs + h * half_rows, half_rows), half_rows)]
 
     q_gain = qn_ref[...].astype(jnp.float32)
-    put(qf, mine_k * heads * seqs, [norm_rope(p, q_gain, cos_full, sin_full) for p in project(0, 1)])
+    put(qf, mine_k * heads * seqs, [norm_rope(p, q_gain, cos_full, sin_full) for p in project(0, 2)])
     arrived()
     count = 0
     sent = []
@@ -147,7 +147,7 @@
     own = [[push(q_half(mine_k, h), peer) for peer in (right, left)] for h in range(2)]
     push(q_half(mine_k, 0), partner)
     push(q_half(mine_k, 1), partner)
-    put(qf, k_opp * heads * seqs, [norm_rope(p, q_gain, cos_full, sin_full) for p in project(1, 2)])
+    put(qf, k_opp * heads * seqs, [norm_rope(p, q_gain, cos_full, sin_full) for p in project(1, 4)])
     push(q_half(k_opp, 0), partner)
     push(q_half(k_opp, 1), partner)
 
@@ -214,7 +214,7 @@
 
 
 def attend_kernel(pos_in, qf, kf, vf, k_in, v_in, ko_ref, vo_ref, new_out, part_ref, kbuf, vbuf,
-                  pos_ref, new_ref, mstat, lstat, sbuf, ebuf, obuf, possem, newsem, kosem, vosem):
+                  pos_ref, new_ref, mstat, lstat, sbuf, ebuf, possem, newsem, kosem, vosem):
     seqs, slots, kv_heads, head_dim = kbuf.shape
     groups = kosem.shape[0]
     per_group = seqs // groups
@@ -275,10 +275,8 @@
             m_acc = jnp.where(lane == b, m, m_acc)
             l_acc = jnp.where(lane == b, l, l_acc)
         for bb, b in enumerate(members):
-            obuf[bb] = jnp.dot(ebuf[bb], vbuf[b].reshape(cols, head_dim), preferred_element_type=jnp.float32)
-        for bb, b in enumerate(members):
-            for h in range(q_heads):
-                part_ref[h, pl.ds(b, 1), :] = obuf[bb, h:h + 1, :]
+            o = jnp.dot(ebuf[bb], vbuf[b].reshape(cols, head_dim), preferred_element_type=jnp.float32)
+            part_ref[pl.ds(b, q_heads, stride=seqs + STAT_ROWS), :] = o
         mstat[...] = m_acc
         lstat[...] = l_acc
         return carry
@@ -286,9 +284,10 @@
     lax.fori_loop(0, groups, group_step, 0)
 
     for h in range(q_heads):
-        part_ref[h, seqs:seqs + 1, :] = mstat[h:h + 1, :]
-        part_ref[h, seqs + 1:seqs + 2, :] = lstat[h:h + 1, :]
-        part_ref[h, seqs + 2:seqs + STAT_ROWS, :] = jnp.zeros((STAT_ROWS - 2, 128), jnp.float32)
+        row = h * (seqs + STAT_ROWS) + seqs
+        part_ref[row:row + 1, :] = mstat[h:h + 1, :]
+        part_ref[row + 1:row + 2, :] = lstat[h:h + 1, :]
+        part_ref[row + 2:row + STAT_ROWS, :] = jnp.zeros((STAT_ROWS - 2, 128), jnp.float32)
     for g in range(groups):
         for copy in writes(g):
             copy.wait()
@@ -297,7 +296,7 @@
 def attend_stage(positions, qf, kf, vf, k_vm, v_vm):
     seqs, slots, kv_heads, head_dim = k_vm.shape
     q_heads = qf.shape[0] // seqs
-    groups = 8
+    groups = 4
     vmem = pl.BlockSpec(memory_space=pltpu.VMEM)
     anyspec = pl.BlockSpec(memory_space=pl.ANY)
     hbm = pl.BlockSpec(memory_space=pltpu.HBM)
@@ -309,7 +308,7 @@
             jax.ShapeDtypeStruct(k_vm.shape, k_vm.dtype),
             jax.ShapeDtypeStruct(v_vm.shape, v_vm.dtype),
             jax.ShapeDtypeStruct((seqs, 2, kv_heads, head_dim), jnp.bfloat16),
-            pltpu.VMEM((q_heads, seqs + STAT_ROWS, head_dim), jnp.float32),
+            pltpu.VMEM((q_heads * (seqs + STAT_ROWS), head_dim), jnp.float32),
             pltpu.VMEM(k_vm.shape, k_vm.dtype),
             pltpu.VMEM(v_vm.shape, v_vm.dtype),
         ),
@@ -323,7 +322,6 @@
             pltpu.VMEM((q_heads, 128), jnp.float32),
             pltpu.VMEM((seqs // groups, q_heads, slots * kv_heads), jnp.float32),
             pltpu.VMEM((seqs // groups, q_heads, slots * kv_heads), jnp.bfloat16),
-            pltpu.VMEM((seqs // groups, q_heads, head_dim), jnp.float32),
             dma, dma((groups,)), dma((groups,)), dma((groups,)),
         ],
         compiler_params=pltpu.CompilerParams(vmem_limit_bytes=16 * 1024 * 1024),
@@ -363,6 +361,9 @@
     def wo_copy(k):
         return pltpu.make_async_copy(wo_ref.at[pl.ds(pl.multiple_of(k * k_rows, k_rows), k_rows)], wov.at[k], wsem.at[k])
 
+    other = (1 - core) * 4
+    for k in [core * 4 + q for q in keep] + [other + q for q in keep] + [core * 4 + q for q in give] + [other + q for q in give]:
+        wo_copy(k).start()
     arrived()
     sent = []
 
@@ -370,33 +371,36 @@
         sent.append(send(src, dst, ss, rs, peer))
         return sent[-1]
 
-    order = give + keep
     heads = per * 4
-    pair = [push(mine.at[pl.ds((1 - core) * heads + q * per, per)], pin.at[i], s0.at[i], r0.at[i], partner)
-            for i, q in enumerate(order)]
-    for k in range(2):
-        wo_copy(k).start()
+    size = seqs + STAT_ROWS
+
+    def part_of(ref, h, count=1):
+        return ref.at[pl.ds(pl.multiple_of(h * size, 8), count * size)]
+
+    pair = [[push(part_of(mine, (1 - core) * heads + give[c] * per + i), pin.at[c, i], s0.at[c, i], r0.at[c, i], partner)
+             for c in range(2)] for i in range(per)]
+    pair_keep = [[push(part_of(mine, (1 - core) * heads + keep[c] * per + i), pin.at[2 + c, i], s0.at[2 + c, i], r0.at[2 + c, i], partner)
+                  for c in range(2)] for i in range(per)]
 
     def put(dst, merged):
         rows, stat = merged
         dst[0:seqs, :] = rows
         dst[seqs:seqs + STAT_ROWS, :] = stat
 
-    pair[0].wait_recv()
-    pair[1].wait_recv()
     step1 = [[], []]
     for i in range(per):
         for c in range(2):
-            put(away.at[c, i], merge([mine.at[core * heads + give[c] * per + i], pin.at[c, i]], seqs))
+            pair[i][c].wait_recv()
+        for c in range(2):
+            put(away.at[c, i], merge([part_of(mine, core * heads + give[c] * per + i), pin.at[c, i]], seqs))
         for c in range(2):
             step1[c].append(push(away.at[c, i], in1.at[c, i], s1.at[c, i], r1.at[c, i], first[c]))
-    for k in range(2, 8):
-        wo_copy(k).start()
-    pair[2].wait_recv()
-    pair[3].wait_recv()
+    for copies in pair_keep:
+        for copy in copies:
+            copy.wait_recv()
     for i in range(per):
         for c in range(2):
-            put(kept.at[c, i], merge([mine.at[core * heads + keep[c] * per + i], pin.at[2 + c, i]], seqs))
+            put(kept.at[c, i], merge([part_of(mine, core * heads + keep[c] * per + i), pin.at[2 + c, i]], seqs))
     step2 = [[], []]
     for i in range(per):
         for c in range(2):
@@ -432,35 +436,53 @@
             y = jnp.dot(lhs, wov[k, :, off], preferred_element_type=jnp.float32)
             res[:, off] = y if fresh else res[:, off] + y
 
-    other = (1 - core) * 4
+    def multiply_pair(base, i, last=False):
+        ks = [base + give[c] for c in range(2)]
+        if i == 0:
+            for k in ks:
+                wo_copy(k).wait()
+        part = slice(i * seqs, (i + 1) * seqs)
+        depth = slice(i * (k_rows // per), (i + 1) * (k_rows // per))
+        lhs = jnp.concatenate([att[k, part, :] for k in ks], axis=1).astype(jnp.bfloat16)
+        for j in range(model // cols):
+            off = slice(j * cols, (j + 1) * cols)
+            rhs = jnp.concatenate([wov[k, depth, off] for k in ks], axis=0)
+            y = res[:, off] + jnp.dot(lhs, rhs, preferred_element_type=jnp.float32)
+            if last:
+                out_ref[:, off] = (tok_ref[:, off].astype(jnp.float32) + y).astype(jnp.bfloat16)
+            else:
+                res[:, off] = y
+
     multiply(blocks[0], fresh=True)
     multiply(blocks[1])
     for c in range(2):
         for i in range(per):
             own[c][i].wait_recv()
         multiply(other + keep[c])
-    passed = [[], []]
+    tok_copy.wait()
+    passed = []
     for i in range(per):
         for c in range(2):
             step3[c][i].wait_recv()
             piece = rows_of(core * 4 + give[c], i)
-            passed[c].append(push(piece, piece, s5.at[c, i], r5.at[c, i], partner))
-    for c in range(2):
-        multiply(core * 4 + give[c])
-    for c in range(2):
-        for i in range(per):
-            passed[c][i].wait_recv()
-        multiply(other + give[c])
-    tok_copy.wait()
-    out_ref[...] = (tok_ref[...].astype(jnp.float32) + res[...]).astype(jnp.bfloat16)
+            passed.append(push(piece, piece, s5.at[c, i], r5.at[c, i], partner))
+        multiply_pair(core * 4, i)
+        if i > 0:
+            for copy in passed[2 * i - 2:2 * i]:
+                copy.wait_recv()
+            multiply_pair(other, i - 1)
+    for copy in passed[2 * per - 2:]:
+        copy.wait_recv()
+    multiply_pair(other, per - 1, last=True)
     for copy in sent:
         copy.wait_send()
 
 
 def tail_stage(part, w_o, tokens, group):
     seqs, model = tokens.shape
-    q_heads, rows, head_dim = part.shape
-    per = q_heads // group
+    head_dim = part.shape[-1]
+    rows = seqs + STAT_ROWS
+    per = part.shape[0] // rows // group
     vmem = pl.BlockSpec(memory_space=pltpu.VMEM)
     hbm = pl.BlockSpec(memory_space=pltpu.HBM)
     dma = pltpu.SemaphoreType.DMA
@@ -479,7 +501,7 @@
             pltpu.VMEM((group, per * seqs, head_dim), jnp.float32),
             pltpu.VMEM((group, w_o.shape[0] // group, model), jnp.bfloat16),
             pltpu.VMEM((seqs, model), jnp.float32),
-            dma((group,)), dma((4,)), dma((4,)),
+            dma((group,)), dma((4, per)), dma((4, per)),
         ] + [dma((2, per))] * 10,
         compiler_params=pltpu.CompilerParams(collective_id=0, has_side_effects=True, vmem_limit_bytes=44 * 1024 * 1024),
     )(part, *in_hbm(w_o, tokens))

time: 45 us -> 44.6 us (level)
  Pallas kernels: 43.5 us -> 43 us
    pallas_call x1, Pallas kernels: 7.68 us -> 6.83 us  [attend_stage(): pl.pallas_call(attend_kernel, name='attend_stage', out_shape=(jax.ShapeDt...]
where the time goes in v6:
time: 44.6 us; the launch traced here: 44.5 us
  Pallas kernels  43 us (96%)
  local copies, waits for them, and re-layouts  0.8 us (2%)
  between operations  0.66 us (1%)
    pallas_call x1, Pallas kernels, tail_stage(): pl.pallas_call(tail_kernel, name='tail_stage', out_shape=pltpu.VMEM((seqs...  21.6 us
    pallas_call x1, Pallas kernels, project_stage(): pl.pallas_call(project_kernel, name='project_stage', out_shape=(pltpu.VME...  14.6 us
    pallas_call x1, Pallas kernels, attend_stage(): pl.pallas_call(attend_kernel, name='attend_stage', out_shape=(jax.ShapeDt...  6.83 us

profile of v6, /device:TPU:113, one launch (start us, length us, event | category | flops | bytes accessed | tf_op | source)
XLA Modules:
  0.0 44.5 jit_solution(6432208468202022912)
XLA Ops:
  0.6 14.6 %project_stage.1 = (f32[2048,128]{1,0:T(8,128)S(1)}, f32[512,128]{1,0:T(8,128)S(1)}, f32[512,128]{1,0:T(8,128)S(1)}, bf16[64,64,8,128]{3,2,1,0:T(8,128)(2,1)S(1)}, bf16[64,64,8,128]{3,2,1,0:T(8,128)(2,1)S(1)}) custom-call(s32[64]{0:T(128)} %pos_in.3, bf16[64,4096]{1,0:T(8,128)(2,1)} %tok_in.3, f32[1,128]{1,0:T(1,128)} %constant.2.clone.freq_in, ...), custom_call_target="tpu_custom_call" | custom-call | tf_op jit(solution)/shard_map/project_stage/pallas_call | solution.py:186
  15.2 6.8 %attend_stage.1 = (bf16[64,64,8,128]{3,2,1,0:T(8,128)(2,1)}, bf16[64,64,8,128]{3,2,1,0:T(8,128)(2,1)}, bf16[64,2,8,128]{3,2,1,0:T(8,128)(2,1)}, f32[2304,128]{1,...) custom-call(s32[64]{0:T(128)} %pos_in.3, ...), custom_call_target="tpu_custom_call", output_to_operand_aliasing={{4}: (4, {}), {5}: (5, {})} | custom-call | tf_op jit(solution)/shard_map/attend_stage/pallas_call | solution.py:304
  22.1 21.6 %tail_stage.1 = bf16[64,4096]{1,0:T(8,128)(2,1)S(1)} custom-call(f32[2304,128]{1,0:T(8,128)S(1)} %get-tuple-element.18.mine, bf16[4096,4096]{1,0:T(8,128)(2,1)} %wo_ref.1, bf16[64,4096]{1,0:T(8,128)(2,1)} %tok_in.3), custom_call_target="tpu_custom_call" | custom-call | tf_op jit(solution)/shard_map/tail_stage/pallas_call | solution.py:490
  43.7 0.8 %copy.21 = bf16[64,4096]{1,0:T(8,128)(2,1)} copy(bf16[64,4096]{1,0:T(8,128)(2,1)S(1)} %tail_stage.1) | data formatting | bytes 1048576

commit v7 on v6

--- a/solution.py
+++ b/solution.py
@@ -13,6 +13,7 @@
 NEG_FILL = -1e30
 MESH = pl.DeviceIdType.MESH
 STAT_ROWS = 8
+PIECES = 2
 
 
 def in_hbm(*arrays):
@@ -127,10 +128,8 @@
         for h, value in enumerate(values):
             dst[pl.ds(pl.multiple_of(base + h * seqs, seqs), seqs), :] = value
 
-    half_rows = heads // 2 * seqs
-
-    def q_half(k, h):
-        return qf.at[pl.ds(pl.multiple_of(k * heads * seqs + h * half_rows, half_rows), half_rows)]
+    def q_chunk(k):
+        return qf.at[pl.ds(pl.multiple_of(k * heads * seqs, heads * seqs), heads * seqs)]
 
     q_gain = qn_ref[...].astype(jnp.float32)
     put(qf, mine_k * heads * seqs, [norm_rope(p, q_gain, cos_full, sin_full) for p in project(0, 2)])
@@ -144,12 +143,10 @@
         count += 1
         return sent[-1]
 
-    own = [[push(q_half(mine_k, h), peer) for peer in (right, left)] for h in range(2)]
-    push(q_half(mine_k, 0), partner)
-    push(q_half(mine_k, 1), partner)
+    own = [push(q_chunk(mine_k), peer) for peer in (right, left)]
+    push(q_chunk(mine_k), partner)
     put(qf, k_opp * heads * seqs, [norm_rope(p, q_gain, cos_full, sin_full) for p in project(1, 4)])
-    push(q_half(k_opp, 0), partner)
-    push(q_half(k_opp, 1), partner)
+    push(q_chunk(k_opp), partner)
 
     kv_rows = heads * seqs
     kv_base = core * kv_rows
@@ -161,13 +158,11 @@
     push(vf.at[kv_part], partner)
     issue(len(bulk) - issued)
 
-    for h in range(2):
-        for from_peer, k in zip(own[h], (k_left, k_right)):
-            from_peer.wait_recv()
-            push(q_half(k, h), partner)
-    waited = own[0] + own[1]
+    for from_peer, k in zip(own, (k_left, k_right)):
+        from_peer.wait_recv()
+        push(q_chunk(k), partner)
     for copy in sent:
-        if not any(copy is w for w in waited):
+        if not any(copy is w for w in own):
             copy.wait_recv()
         copy.wait_send()
     for copy in bulk[4 * blocks:]:
@@ -345,7 +340,9 @@
 def tail_kernel(mine, wo_ref, tok_in, out_ref, tok_ref, toksem, pin, away, kept, in1, out2, in2, att, wov, res,
                 wsem, s0, r0, s1, r1, s2, r2, s3, r3, s4, r4, s5, r5):
     seqs, model = tok_ref.shape
-    per = away.shape[1]
+    size = seqs + STAT_ROWS
+    per = away.shape[1] // size
+    hp = per // PIECES
     tok_copy = pltpu.make_async_copy(tok_in, tok_ref, toksem)
     tok_copy.start()
     chips, core, chip, _, _, _, partner, _, _ = ring_place()
@@ -372,58 +369,66 @@
         return sent[-1]
 
     heads = per * 4
-    size = seqs + STAT_ROWS
 
     def part_of(ref, h, count=1):
         return ref.at[pl.ds(pl.multiple_of(h * size, 8), count * size)]
 
-    pair = [[push(part_of(mine, (1 - core) * heads + give[c] * per + i), pin.at[c, i], s0.at[c, i], r0.at[c, i], partner)
-             for c in range(2)] for i in range(per)]
-    pair_keep = [[push(part_of(mine, (1 - core) * heads + keep[c] * per + i), pin.at[2 + c, i], s0.at[2 + c, i], r0.at[2 + c, i], partner)
-                  for c in range(2)] for i in range(per)]
-
-    def put(dst, merged):
+    def piece_of(ref, i):
+        return part_of(ref, i * hp, hp)
+
+    def trade(q, slot, i):
+        return push(part_of(mine, (1 - core) * heads + q * per + i * hp, hp), piece_of(pin.at[slot], i), s0.at[slot, i], r0.at[slot, i], partner)
+
+    pair = [[trade(give[c], c, i) for c in range(2)] for i in range(PIECES)]
+    pair_keep = [[trade(keep[c], 2 + c, i) for c in range(2)] for i in range(PIECES)]
+
+    def put(dst, h, merged):
         rows, stat = merged
-        dst[0:seqs, :] = rows
-        dst[seqs:seqs + STAT_ROWS, :] = stat
+        dst[h * size:h * size + seqs, :] = rows
+        dst[h * size + seqs:(h + 1) * size, :] = stat
+
+    def members(i):
+        return [(h, c) for h in range(i * hp, (i + 1) * hp) for c in range(2)]
 
     step1 = [[], []]
-    for i in range(per):
+    for i in range(PIECES):
         for c in range(2):
             pair[i][c].wait_recv()
-        for c in range(2):
-            put(away.at[c, i], merge([part_of(mine, core * heads + give[c] * per + i), pin.at[c, i]], seqs))
-        for c in range(2):
-            step1[c].append(push(away.at[c, i], in1.at[c, i], s1.at[c, i], r1.at[c, i], first[c]))
+        for h, c in members(i):
+            put(away.at[c], h, merge([part_of(mine, core * heads + give[c] * per + h), part_of(pin.at[c], h)], seqs))
+        for c in range(2):
+            step1[c].append(push(piece_of(away.at[c], i), piece_of(in1.at[c], i), s1.at[c, i], r1.at[c, i], first[c]))
     for copies in pair_keep:
         for copy in copies:
             copy.wait_recv()
-    for i in range(per):
-        for c in range(2):
-            put(kept.at[c, i], merge([part_of(mine, core * heads + keep[c] * per + i), pin.at[2 + c, i]], seqs))
+    for i in range(PIECES):
+        for h, c in members(i):
+            put(kept.at[c], h, merge([part_of(mine, core * heads + keep[c] * per + h), part_of(pin.at[2 + c], h)], seqs))
     step2 = [[], []]
-    for i in range(per):
+    for i in range(PIECES):
         for c in range(2):
             step1[c][i].wait_recv()
-        for c in range(2):
-            put(out2.at[c, i], merge([kept.at[c, i], in1.at[c, i]], seqs))
-        for c in range(2):
-            step2[c].append(push(out2.at[c, i], in2.at[c, i], s2.at[c, i], r2.at[c, i], second[c]))
+        for h, c in members(i):
+            put(out2.at[c], h, merge([part_of(kept.at[c], h), part_of(in1.at[c], h)], seqs))
+        for c in range(2):
+            step2[c].append(push(piece_of(out2.at[c], i), piece_of(in2.at[c], i), s2.at[c, i], r2.at[c, i], second[c]))
     step3, own = [[], []], [[], []]
     blocks = [core * 4 + keep[c] for c in range(2)]
 
     def rows_of(k, i):
-        return att.at[k, pl.ds(i * seqs, seqs)]
-
-    for i in range(per):
+        return att.at[k, pl.ds(i * hp * seqs, hp * seqs)]
+
+    for i in range(PIECES):
         for c in range(2):
             step2[c][i].wait_recv()
-        for c in range(2):
-            done = merge([out2.at[c, i], in2.at[c, i]], seqs, final=True)
-            att[blocks[c], i * seqs:(i + 1) * seqs, :] = done.astype(jnp.bfloat16).astype(jnp.float32)
+        for h, c in members(i):
+            done = merge([part_of(out2.at[c], h), part_of(in2.at[c], h)], seqs, final=True)
+            att[blocks[c], h * seqs:(h + 1) * seqs, :] = done.astype(jnp.bfloat16).astype(jnp.float32)
         for c in range(2):
             piece = rows_of(blocks[c], i)
             step3[c].append(push(piece, piece, s3.at[c, i], r3.at[c, i], first[c]))
+        for c in range(2):
+            piece = rows_of(blocks[c], i)
             own[c].append(push(piece, piece, s4.at[c, i], r4.at[c, i], partner))
 
     cols = 512
@@ -441,9 +446,8 @@
         if i == 0:
             for k in ks:
                 wo_copy(k).wait()
-        part = slice(i * seqs, (i + 1) * seqs)
-        depth = slice(i * (k_rows // per), (i + 1) * (k_rows // per))
-        lhs = jnp.concatenate([att[k, part, :] for k in ks], axis=1).astype(jnp.bfloat16)
+        depth = slice(i * (k_rows // PIECES), (i + 1) * (k_rows // PIECES))
+        lhs = jnp.concatenate([att[k, h * seqs:(h + 1) * seqs, :] for k in ks for h in range(i * hp, (i + 1) * hp)], axis=1).astype(jnp.bfloat16)
         for j in range(model // cols):
             off = slice(j * cols, (j + 1) * cols)
             rhs = jnp.concatenate([wov[k, depth, off] for k in ks], axis=0)
@@ -456,12 +460,12 @@
     multiply(blocks[0], fresh=True)
     multiply(blocks[1])
     for c in range(2):
-        for i in range(per):
+        for i in range(PIECES):
             own[c][i].wait_recv()
         multiply(other + keep[c])
     tok_copy.wait()
     passed = []
-    for i in range(per):
+    for i in range(PIECES):
         for c in range(2):
             step3[c][i].wait_recv()
             piece = rows_of(core * 4 + give[c], i)
@@ -471,9 +475,9 @@
             for copy in passed[2 * i - 2:2 * i]:
                 copy.wait_recv()
             multiply_pair(other, i - 1)
-    for copy in passed[2 * per - 2:]:
+    for copy in passed[2 * PIECES - 2:]:
         copy.wait_recv()
-    multiply_pair(other, per - 1, last=True)
+    multiply_pair(other, PIECES - 1, last=True)
     for copy in sent:
         copy.wait_send()
 
@@ -486,7 +490,7 @@
     vmem = pl.BlockSpec(memory_space=pltpu.VMEM)
     hbm = pl.BlockSpec(memory_space=pltpu.HBM)
     dma = pltpu.SemaphoreType.DMA
-    sums = pltpu.VMEM((2, per, rows, head_dim), jnp.float32)
+    sums = pltpu.VMEM((2, per * rows, head_dim), jnp.float32)
     return pl.pallas_call(
         tail_kernel,
         name='tail_stage',
@@ -496,13 +500,13 @@
         scratch_shapes=[
             pltpu.VMEM((seqs, model), tokens.dtype),
             dma,
-            pltpu.VMEM((4, per, rows, head_dim), jnp.float32),
+            pltpu.VMEM((4, per * rows, head_dim), jnp.float32),
             sums, sums, sums, sums, sums,
             pltpu.VMEM((group, per * seqs, head_dim), jnp.float32),
             pltpu.VMEM((group, w_o.shape[0] // group, model), jnp.bfloat16),
             pltpu.VMEM((seqs, model), jnp.float32),
-            dma((group,)), dma((4, per)), dma((4, per)),
-        ] + [dma((2, per))] * 10,
+            dma((group,)), dma((4, PIECES)), dma((4, PIECES)),
+        ] + [dma((2, PIECES))] * 10,
         compiler_params=pltpu.CompilerParams(collective_id=0, has_side_effects=True, vmem_limit_bytes=44 * 1024 * 1024),
     )(part, *in_hbm(w_o, tokens))
 

time: 44.6 us -> 45.5 us (1.020)
  Pallas kernels: 43 us -> 44 us
    pallas_call x1, Pallas kernels: 21.6 us -> 22.4 us  [tail_stage(): pl.pallas_call(tail_kernel, name='tail_stage', out_shape=pltpu.VMEM((seqs...]
where the time goes in v7:
time: 45.5 us
  Pallas kernels  44 us (97%)
  local copies, waits for them, and re-layouts  0.8 us (2%)
  between operations  0.66 us (1%)
    pallas_call x1, Pallas kernels, tail_stage(): pl.pallas_call(tail_kernel, name='tail_stage', out_shape=pltpu.VMEM((seqs...  22.4 us
    pallas_call x1, Pallas kernels, project_stage(): pl.pallas_call(project_kernel, name='project_stage', out_shape=(pltpu.VME...  14.8 us
    pallas_call x1, Pallas kernels, attend_stage(): pl.pallas_call(attend_kernel, name='attend_stage', out_shape=(jax.ShapeDt...  6.83 us

profile of v7, /device:TPU:113, one launch (start us, length us, event | category | flops | bytes accessed | tf_op | source)
XLA Modules:
  0.0 45.5 jit_solution(17098844869248472354)
XLA Ops:
  0.6 14.8 %project_stage.1 = (f32[2048,128]{1,0:T(8,128)S(1)}, f32[512,128]{1,0:T(8,128)S(1)}, f32[512,128]{1,0:T(8,128)S(1)}, bf16[64,64,8,128]{3,2,1,0:T(8,128)(2,1)S(1)}, bf16[64,64,8,128]{3,2,1,0:T(8,128)(2,1)S(1)}) custom-call(s32[64]{0:T(128)} %pos_in.3, bf16[64,4096]{1,0:T(8,128)(2,1)} %tok_in.3, f32[1,128]{1,0:T(1,128)} %constant.2.clone.freq_in, ...), custom_call_target="tpu_custom_call" | custom-call | tf_op jit(solution)/shard_map/project_stage/pallas_call | solution.py:181
  15.4 6.8 %attend_stage.1 = (bf16[64,64,8,128]{3,2,1,0:T(8,128)(2,1)}, bf16[64,64,8,128]{3,2,1,0:T(8,128)(2,1)}, bf16[64,2,8,128]{3,2,1,0:T(8,128)(2,1)}, f32[2304,128]{1,...) custom-call(s32[64]{0:T(128)} %pos_in.3, ...), custom_call_target="tpu_custom_call", output_to_operand_aliasing={{4}: (4, {}), {5}: (5, {})} | custom-call | tf_op jit(solution)/shard_map/attend_stage/pallas_call | solution.py:299
  22.3 22.4 %tail_stage.1 = bf16[64,4096]{1,0:T(8,128)(2,1)S(1)} custom-call(f32[2304,128]{1,0:T(8,128)S(1)} %get-tuple-element.18.mine, bf16[4096,4096]{1,0:T(8,128)(2,1)} %wo_ref.1, bf16[64,4096]{1,0:T(8,128)(2,1)} %tok_in.3), custom_call_target="tpu_custom_call" | custom-call | tf_op jit(solution)/shard_map/tail_stage/pallas_call | solution.py:494
  44.7 0.8 %copy.21 = bf16[64,4096]{1,0:T(8,128)(2,1)} copy(bf16[64,4096]{1,0:T(8,128)(2,1)S(1)} %tail_stage.1) | data formatting | bytes 1048576

commit v8 on v6

--- a/solution.py
+++ b/solution.py
@@ -251,7 +251,9 @@
     cols = slots * kv_heads
     row_id = lax.broadcasted_iota(jnp.int32, (q_heads, cols), 0)
     col_id = lax.broadcasted_iota(jnp.int32, (q_heads, cols), 1)
-    head_ok = row_id // (q_heads // kv_heads) == col_id % kv_heads
+    head_ok = row_id % kv_heads == col_id % kv_heads
+    q_per = q_heads // kv_heads
+    block_rows = STAT_ROWS + q_per * seqs
     slot_key = jnp.where(head_ok, col_id // kv_heads, slots * 1024)
     lane = lax.broadcasted_iota(jnp.int32, (q_heads, 128), 1)
     score_scale = head_dim ** -0.5
@@ -262,7 +264,7 @@
         m_acc, l_acc = mstat[...], lstat[...]
         members = [g * per_group + bb for bb in range(per_group)]
         for bb, b in enumerate(members):
-            q_b = qf[pl.ds(b, q_heads, stride=seqs), :].astype(jnp.bfloat16)
+            q_b = jnp.concatenate([qf[pl.ds(b + j * seqs, kv_heads, stride=q_per * seqs), :] for j in range(q_per)], axis=0).astype(jnp.bfloat16)
             k_b = kbuf[b].reshape(cols, head_dim)
             sbuf[bb] = lax.dot_general(q_b, k_b, (((1,), (1,)), ((), ())), preferred_element_type=jnp.float32)
         for bb, b in enumerate(members):
@@ -276,18 +278,19 @@
             l_acc = jnp.where(lane == b, l, l_acc)
         for bb, b in enumerate(members):
             o = jnp.dot(ebuf[bb], vbuf[b].reshape(cols, head_dim), preferred_element_type=jnp.float32)
-            part_ref[pl.ds(b, q_heads, stride=seqs + STAT_ROWS), :] = o
+            for j in range(q_per):
+                part_ref[pl.ds(b + STAT_ROWS + j * seqs, kv_heads, stride=block_rows), :] = o[j * kv_heads:(j + 1) * kv_heads, :]
         mstat[...] = m_acc
         lstat[...] = l_acc
         return carry
 
     lax.fori_loop(0, groups, group_step, 0)
 
-    for h in range(q_heads):
-        row = h * (seqs + STAT_ROWS) + seqs
-        part_ref[row:row + 1, :] = mstat[h:h + 1, :]
-        part_ref[row + 1:row + 2, :] = lstat[h:h + 1, :]
-        part_ref[row + 2:row + STAT_ROWS, :] = jnp.zeros((STAT_ROWS - 2, 128), jnp.float32)
+    for k in range(kv_heads):
+        for j in range(q_per):
+            row = k * block_rows + j
+            part_ref[row:row + 1, :] = mstat[j * kv_heads + k:j * kv_heads + k + 1, :]
+            part_ref[row + q_per:row + q_per + 1, :] = lstat[j * kv_heads + k:j * kv_heads + k + 1, :]
     for g in range(groups):
         for copy in writes(g):
             copy.wait()
@@ -308,7 +311,7 @@
             jax.ShapeDtypeStruct(k_vm.shape, k_vm.dtype),
             jax.ShapeDtypeStruct(v_vm.shape, v_vm.dtype),
             jax.ShapeDtypeStruct((seqs, 2, kv_heads, head_dim), jnp.bfloat16),
-            pltpu.VMEM((q_heads * (seqs + STAT_ROWS), head_dim), jnp.float32),
+            pltpu.VMEM((kv_heads * STAT_ROWS + q_heads * seqs, head_dim), jnp.float32),
             pltpu.VMEM(k_vm.shape, k_vm.dtype),
             pltpu.VMEM(v_vm.shape, v_vm.dtype),
         ),
@@ -329,23 +332,25 @@
     return outs[:4]
 
 
-def merge(pieces, seqs, final=False):
-    stats = [jnp.transpose(ref[seqs:seqs + STAT_ROWS, :], (1, 0))[:seqs] for ref in pieces]
-    peak = functools.reduce(jnp.maximum, [t[:, 0:1] for t in stats])
-    factors = [jnp.exp(t[:, 0:1] - peak) for t in stats]
-    total = functools.reduce(jnp.add, [f * t[:, 1:2] for f, t in zip(factors, stats)])
-    rows = functools.reduce(jnp.add, [f * ref[0:seqs, :] for f, ref in zip(factors, pieces)])
-    if final:
-        return rows / total
-    both = jnp.concatenate([peak, total, jnp.zeros((seqs, STAT_ROWS - 2), jnp.float32)], axis=1)
-    both = jnp.concatenate([both, jnp.zeros((128 - seqs, STAT_ROWS), jnp.float32)], axis=0)
-    return rows, jnp.transpose(both, (1, 0))
-
-
-def tail_kernel(mine, wo_ref, tok_in, out_ref, tok_ref, toksem, pin, away, kept, in1, out2, in2, att, wov, res,
+def weigh(tiles, seqs):
+    per = STAT_ROWS // 2
+    stats = [jnp.transpose(tile, (1, 0))[:seqs] for tile in tiles]
+    peak = functools.reduce(jnp.maximum, [t[:, :per] for t in stats])
+    factors = [jnp.exp(t[:, :per] - peak) for t in stats]
+    return factors, peak, functools.reduce(jnp.add, [f * t[:, per:] for f, t in zip(factors, stats)])
+
+
+def stat_tile(peak, total):
+    both = jnp.concatenate([peak, total], axis=1)
+    both = jnp.concatenate([both, jnp.zeros((128 - both.shape[0], STAT_ROWS), jnp.float32)], axis=0)
+    return jnp.transpose(both, (1, 0))
+
+
+def tail_kernel(mine, wo_ref, tok_in, out_ref, tok_ref, toksem, pin, away, in1, out2, in2, att, wov, res,
                 wsem, s0, r0, s1, r1, s2, r2, s3, r3, s4, r4, s5, r5):
     seqs, model = tok_ref.shape
-    per = away.shape[1]
+    size = away.shape[1]
+    per = (size - STAT_ROWS) // seqs
     tok_copy = pltpu.make_async_copy(tok_in, tok_ref, toksem)
     tok_copy.start()
     chips, core, chip, _, _, _, partner, _, _ = ring_place()
@@ -371,45 +376,45 @@
         sent.append(send(src, dst, ss, rs, peer))
         return sent[-1]
 
-    heads = per * 4
-    size = seqs + STAT_ROWS
-
-    def part_of(ref, h, count=1):
-        return ref.at[pl.ds(pl.multiple_of(h * size, 8), count * size)]
-
-    pair = [[push(part_of(mine, (1 - core) * heads + give[c] * per + i), pin.at[c, i], s0.at[c, i], r0.at[c, i], partner)
-             for c in range(2)] for i in range(per)]
-    pair_keep = [[push(part_of(mine, (1 - core) * heads + keep[c] * per + i), pin.at[2 + c, i], s0.at[2 + c, i], r0.at[2 + c, i], partner)
-                  for c in range(2)] for i in range(per)]
-
-    def put(dst, merged):
-        rows, stat = merged
-        dst[0:seqs, :] = rows
-        dst[seqs:seqs + STAT_ROWS, :] = stat
-
-    step1 = [[], []]
-    for i in range(per):
-        for c in range(2):
-            pair[i][c].wait_recv()
-        for c in range(2):
-            put(away.at[c, i], merge([part_of(mine, core * heads + give[c] * per + i), pin.at[c, i]], seqs))
-        for c in range(2):
-            step1[c].append(push(away.at[c, i], in1.at[c, i], s1.at[c, i], r1.at[c, i], first[c]))
-    for copies in pair_keep:
-        for copy in copies:
-            copy.wait_recv()
-    for i in range(per):
-        for c in range(2):
-            put(kept.at[c, i], merge([part_of(mine, core * heads + keep[c] * per + i), pin.at[2 + c, i]], seqs))
-    step2 = [[], []]
-    for i in range(per):
-        for c in range(2):
-            step1[c][i].wait_recv()
-        for c in range(2):
-            put(out2.at[c, i], merge([kept.at[c, i], in1.at[c, i]], seqs))
-        for c in range(2):
-            step2[c].append(push(out2.at[c, i], in2.at[c, i], s2.at[c, i], r2.at[c, i], second[c]))
-    step3, own = [[], []], [[], []]
+    def block_of(k):
+        return mine.at[pl.ds(pl.multiple_of(k * size, 8), size)]
+
+    def piece_of(ref, i):
+        return ref.at[pl.ds(STAT_ROWS + i * seqs, seqs)] if i else ref.at[pl.ds(0, STAT_ROWS + seqs)]
+
+    def trade(q, slot, i):
+        return push(piece_of(block_of((1 - core) * 4 + q), i), piece_of(pin.at[slot], i), s0.at[slot, i], r0.at[slot, i], partner)
+
+    pair = [[trade(give[c], c, i) for c in range(2)] for i in range(per)]
+    pair_keep = [[trade(keep[c], 2 + c, i) for c in range(2)] for i in range(per)]
+
+    def stat(ref):
+        return ref[0:STAT_ROWS, :]
+
+    def blend(refs, factors, h):
+        rows = slice(STAT_ROWS + h * seqs, STAT_ROWS + (h + 1) * seqs)
+        return functools.reduce(jnp.add, [ref[rows, :] * f[:, h:h + 1] for ref, f in zip(refs, factors)])
+
+    def exchange(sources, out, waits, dst, ss, rs, peers):
+        started, factors = [[], []], [None, None]
+        for i in range(per):
+            for c in range(2):
+                for copy in waits(c, i):
+                    copy.wait_recv()
+            for c in range(2):
+                if i == 0:
+                    factors[c], peak, total = weigh([stat(ref) for ref in sources[c]], seqs)
+                    out[c, 0:STAT_ROWS, :] = stat_tile(peak, total)
+                out[c, STAT_ROWS + i * seqs:STAT_ROWS + (i + 1) * seqs, :] = blend(sources[c], factors[c], i)
+            for c in range(2):
+                started[c].append(push(piece_of(out.at[c], i), piece_of(dst.at[c], i), ss.at[c, i], rs.at[c, i], peers[c]))
+        return started
+
+    step1 = exchange([[block_of(core * 4 + give[c]), pin.at[c]] for c in range(2)], away,
+                     lambda c, i: (pair[i][c],), in1, s1, r1, first)
+    step2 = exchange([[block_of(core * 4 + keep[c]), pin.at[2 + c], in1.at[c]] for c in range(2)], out2,
+                     lambda c, i: (pair_keep[i][c], step1[c][i]), in2, s2, r2, second)
+    step3, own, factors = [[], []], [[], []], [None, None]
     blocks = [core * 4 + keep[c] for c in range(2)]
 
     def rows_of(k, i):
@@ -419,11 +424,16 @@
         for c in range(2):
             step2[c][i].wait_recv()
         for c in range(2):
-            done = merge([out2.at[c, i], in2.at[c, i]], seqs, final=True)
-            att[blocks[c], i * seqs:(i + 1) * seqs, :] = done.astype(jnp.bfloat16).astype(jnp.float32)
+            refs = [out2.at[c], in2.at[c]]
+            if i == 0:
+                weights, _, total = weigh([stat(ref) for ref in refs], seqs)
+                factors[c] = [f / total for f in weights]
+            att[blocks[c], i * seqs:(i + 1) * seqs, :] = blend(refs, factors[c], i).astype(jnp.bfloat16).astype(jnp.float32)
         for c in range(2):
             piece = rows_of(blocks[c], i)
             step3[c].append(push(piece, piece, s3.at[c, i], r3.at[c, i], first[c]))
+        for c in range(2):
+            piece = rows_of(blocks[c], i)
             own[c].append(push(piece, piece, s4.at[c, i], r4.at[c, i], partner))
 
     cols = 512
@@ -481,12 +491,12 @@
 def tail_stage(part, w_o, tokens, group):
     seqs, model = tokens.shape
     head_dim = part.shape[-1]
-    rows = seqs + STAT_ROWS
-    per = part.shape[0] // rows // group
+    rows = part.shape[0] // group
+    per = (rows - STAT_ROWS) // seqs
     vmem = pl.BlockSpec(memory_space=pltpu.VMEM)
     hbm = pl.BlockSpec(memory_space=pltpu.HBM)
     dma = pltpu.SemaphoreType.DMA
-    sums = pltpu.VMEM((2, per, rows, head_dim), jnp.float32)
+    sums = pltpu.VMEM((2, rows, head_dim), jnp.float32)
     return pl.pallas_call(
         tail_kernel,
         name='tail_stage',
@@ -496,8 +506,8 @@
         scratch_shapes=[
             pltpu.VMEM((seqs, model), tokens.dtype),
             dma,
-            pltpu.VMEM((4, per, rows, head_dim), jnp.float32),
-            sums, sums, sums, sums, sums,
+            pltpu.VMEM((4, rows, head_dim), jnp.float32),
+            sums, sums, sums, sums,
             pltpu.VMEM((group, per * seqs, head_dim), jnp.float32),
             pltpu.VMEM((group, w_o.shape[0] // group, model), jnp.bfloat16),
             pltpu.VMEM((seqs, model), jnp.float32),

time: 44.6 us -> 44.4 us (level)
  no operation moved by 1% of the time
where the time goes in v8:
time: 44.4 us
  Pallas kernels  42.9 us (97%)
  local copies, waits for them, and re-layouts  0.8 us (2%)
  between operations  0.66 us (1%)
    pallas_call x1, Pallas kernels, tail_stage(): pl.pallas_call(tail_kernel, name='tail_stage', out_shape=pltpu.VMEM((seqs...  21.5 us
    pallas_call x1, Pallas kernels, project_stage(): pl.pallas_call(project_kernel, name='project_stage', out_shape=(pltpu.VME...  14.6 us
    pallas_call x1, Pallas kernels, attend_stage(): pl.pallas_call(attend_kernel, name='attend_stage', out_shape=(jax.ShapeDt...  6.83 us

profile of v8, /device:TPU:113, one launch (start us, length us, event | category | flops | bytes accessed | tf_op | source)
XLA Modules:
  0.0 44.4 jit_solution(804931656480665595)
XLA Ops:
  0.6 14.6 %project_stage.1 = (f32[2048,128]{1,0:T(8,128)S(1)}, f32[512,128]{1,0:T(8,128)S(1)}, f32[512,128]{1,0:T(8,128)S(1)}, bf16[64,64,8,128]{3,2,1,0:T(8,128)(2,1)S(1)}, bf16[64,64,8,128]{3,2,1,0:T(8,128)(2,1)S(1)}) custom-call(s32[64]{0:T(128)} %pos_in.3, bf16[64,4096]{1,0:T(8,128)(2,1)} %tok_in.3, f32[1,128]{1,0:T(1,128)} %constant.2.clone.freq_in, ...), custom_call_target="tpu_custom_call" | custom-call | tf_op jit(solution)/shard_map/project_stage/pallas_call | solution.py:186
  15.2 6.8 %attend_stage.1 = (bf16[64,64,8,128]{3,2,1,0:T(8,128)(2,1)}, bf16[64,64,8,128]{3,2,1,0:T(8,128)(2,1)}, bf16[64,2,8,128]{3,2,1,0:T(8,128)(2,1)}, f32[2112,128]{1,...) custom-call(s32[64]{0:T(128)} %pos_in.3, ...), custom_call_target="tpu_custom_call", output_to_operand_aliasing={{4}: (4, {}), {5}: (5, {})} | custom-call | tf_op jit(solution)/shard_map/attend_stage/pallas_call | solution.py:307
  22.1 21.5 %tail_stage.1 = bf16[64,4096]{1,0:T(8,128)(2,1)S(1)} custom-call(f32[2112,128]{1,0:T(8,128)S(1)} %get-tuple-element.18.mine, bf16[4096,4096]{1,0:T(8,128)(2,1)} %wo_ref.1, bf16[64,4096]{1,0:T(8,128)(2,1)} %tok_in.3), custom_call_target="tpu_custom_call" | custom-call | tf_op jit(solution)/shard_map/tail_stage/pallas_call | solution.py:500
  43.6 0.8 %copy.21 = bf16[64,4096]{1,0:T(8,128)(2,1)} copy(bf16[64,4096]{1,0:T(8,128)(2,1)S(1)} %tail_stage.1) | data formatting | bytes 1048576

commit v9 on v8

--- a/solution.py
+++ b/solution.py
@@ -388,16 +388,22 @@
     pair = [[trade(give[c], c, i) for c in range(2)] for i in range(per)]
     pair_keep = [[trade(keep[c], 2 + c, i) for c in range(2)] for i in range(per)]
 
+    part_rows = seqs // 2
+
+    def bit_of(ref, i):
+        return ref.at[pl.ds(STAT_ROWS + i * part_rows, part_rows)] if i else ref.at[pl.ds(0, STAT_ROWS + part_rows)]
+
     def stat(ref):
         return ref[0:STAT_ROWS, :]
 
-    def blend(refs, factors, h):
-        rows = slice(STAT_ROWS + h * seqs, STAT_ROWS + (h + 1) * seqs)
-        return functools.reduce(jnp.add, [ref[rows, :] * f[:, h:h + 1] for ref, f in zip(refs, factors)])
+    def blend(refs, factors, i):
+        rows = slice(STAT_ROWS + i * part_rows, STAT_ROWS + (i + 1) * part_rows)
+        seq = slice(i % 2 * part_rows, (i % 2 + 1) * part_rows)
+        return functools.reduce(jnp.add, [ref[rows, :] * f[seq, i // 2:i // 2 + 1] for ref, f in zip(refs, factors)])
 
     def exchange(sources, out, waits, dst, ss, rs, peers):
         started, factors = [[], []], [None, None]
-        for i in range(per):
+        for i in range(2 * per):
             for c in range(2):
                 for copy in waits(c, i):
                     copy.wait_recv()
@@ -405,36 +411,38 @@
                 if i == 0:
                     factors[c], peak, total = weigh([stat(ref) for ref in sources[c]], seqs)
                     out[c, 0:STAT_ROWS, :] = stat_tile(peak, total)
-                out[c, STAT_ROWS + i * seqs:STAT_ROWS + (i + 1) * seqs, :] = blend(sources[c], factors[c], i)
+                out[c, STAT_ROWS + i * part_rows:STAT_ROWS + (i + 1) * part_rows, :] = blend(sources[c], factors[c], i)
             for c in range(2):
-                started[c].append(push(piece_of(out.at[c], i), piece_of(dst.at[c], i), ss.at[c, i], rs.at[c, i], peers[c]))
+                started[c].append(push(bit_of(out.at[c], i), bit_of(dst.at[c], i), ss.at[c, i], rs.at[c, i], peers[c]))
         return started
 
     step1 = exchange([[block_of(core * 4 + give[c]), pin.at[c]] for c in range(2)], away,
-                     lambda c, i: (pair[i][c],), in1, s1, r1, first)
+                     lambda c, i: () if i % 2 else (pair[i // 2][c],), in1, s1, r1, first)
     step2 = exchange([[block_of(core * 4 + keep[c]), pin.at[2 + c], in1.at[c]] for c in range(2)], out2,
-                     lambda c, i: (pair_keep[i][c], step1[c][i]), in2, s2, r2, second)
+                     lambda c, i: (step1[c][i],) if i % 2 else (pair_keep[i // 2][c], step1[c][i]), in2, s2, r2, second)
     step3, own, factors = [[], []], [[], []], [None, None]
     blocks = [core * 4 + keep[c] for c in range(2)]
 
     def rows_of(k, i):
         return att.at[k, pl.ds(i * seqs, seqs)]
 
-    for i in range(per):
+    for i in range(2 * per):
         for c in range(2):
             step2[c][i].wait_recv()
+        rows = slice(i * part_rows, (i + 1) * part_rows)
         for c in range(2):
             refs = [out2.at[c], in2.at[c]]
             if i == 0:
                 weights, _, total = weigh([stat(ref) for ref in refs], seqs)
                 factors[c] = [f / total for f in weights]
-            att[blocks[c], i * seqs:(i + 1) * seqs, :] = blend(refs, factors[c], i).astype(jnp.bfloat16).astype(jnp.float32)
+            att[blocks[c], rows, :] = blend(refs, factors[c], i).astype(jnp.bfloat16).astype(jnp.float32)
         for c in range(2):
-            piece = rows_of(blocks[c], i)
+            piece = att.at[blocks[c], pl.ds(i * part_rows, part_rows)]
             step3[c].append(push(piece, piece, s3.at[c, i], r3.at[c, i], first[c]))
-        for c in range(2):
-            piece = rows_of(blocks[c], i)
-            own[c].append(push(piece, piece, s4.at[c, i], r4.at[c, i], partner))
+        if i % 2:
+            for c in range(2):
+                piece = rows_of(blocks[c], i // 2)
+                own[c].append(push(piece, piece, s4.at[c, i // 2], r4.at[c, i // 2], partner))
 
     cols = 512
 
@@ -473,7 +481,8 @@
     passed = []
     for i in range(per):
         for c in range(2):
-            step3[c][i].wait_recv()
+            step3[c][2 * i].wait_recv()
+            step3[c][2 * i + 1].wait_recv()
             piece = rows_of(core * 4 + give[c], i)
             passed.append(push(piece, piece, s5.at[c, i], r5.at[c, i], partner))
         multiply_pair(core * 4, i)
@@ -512,7 +521,7 @@
             pltpu.VMEM((group, w_o.shape[0] // group, model), jnp.bfloat16),
             pltpu.VMEM((seqs, model), jnp.float32),
             dma((group,)), dma((4, per)), dma((4, per)),
-        ] + [dma((2, per))] * 10,
+        ] + [dma((2, 2 * per))] * 10,
         compiler_params=pltpu.CompilerParams(collective_id=0, has_side_effects=True, vmem_limit_bytes=44 * 1024 * 1024),
     )(part, *in_hbm(w_o, tokens))
 

time: 44.4 us -> 44.6 us (level)
  no operation moved by 1% of the time
where the time goes in v9:
time: 44.6 us
  Pallas kernels  43.1 us (97%)
  local copies, waits for them, and re-layouts  0.8 us (2%)
  between operations  0.66 us (1%)
    pallas_call x1, Pallas kernels, tail_stage(): pl.pallas_call(tail_kernel, name='tail_stage', out_shape=pltpu.VMEM((seqs...  21.7 us
    pallas_call x1, Pallas kernels, project_stage(): pl.pallas_call(project_kernel, name='project_stage', out_shape=(pltpu.VME...  14.6 us
    pallas_call x1, Pallas kernels, attend_stage(): pl.pallas_call(attend_kernel, name='attend_stage', out_shape=(jax.ShapeDt...  6.83 us

profile of v9, /device:TPU:113, one launch (start us, length us, event | category | flops | bytes accessed | tf_op | source)
XLA Modules:
  0.0 44.6 jit_solution(1359941411763137814)
XLA Ops:
  0.6 14.6 %project_stage.1 = (f32[2048,128]{1,0:T(8,128)S(1)}, f32[512,128]{1,0:T(8,128)S(1)}, f32[512,128]{1,0:T(8,128)S(1)}, bf16[64,64,8,128]{3,2,1,0:T(8,128)(2,1)S(1)}, bf16[64,64,8,128]{3,2,1,0:T(8,128)(2,1)S(1)}) custom-call(s32[64]{0:T(128)} %pos_in.3, bf16[64,4096]{1,0:T(8,128)(2,1)} %tok_in.3, f32[1,128]{1,0:T(1,128)} %constant.2.clone.freq_in, ...), custom_call_target="tpu_custom_call" | custom-call | tf_op jit(solution)/shard_map/project_stage/pallas_call | solution.py:186
  15.2 6.8 %attend_stage.1 = (bf16[64,64,8,128]{3,2,1,0:T(8,128)(2,1)}, bf16[64,64,8,128]{3,2,1,0:T(8,128)(2,1)}, bf16[64,2,8,128]{3,2,1,0:T(8,128)(2,1)}, f32[2112,128]{1,...) custom-call(s32[64]{0:T(128)} %pos_in.3, ...), custom_call_target="tpu_custom_call", output_to_operand_aliasing={{4}: (4, {}), {5}: (5, {})} | custom-call | tf_op jit(solution)/shard_map/attend_stage/pallas_call | solution.py:307
  22.1 21.7 %tail_stage.1 = bf16[64,4096]{1,0:T(8,128)(2,1)S(1)} custom-call(f32[2112,128]{1,0:T(8,128)S(1)} %get-tuple-element.18.mine, bf16[4096,4096]{1,0:T(8,128)(2,1)} %wo_ref.1, bf16[64,4096]{1,0:T(8,128)(2,1)} %tok_in.3), custom_call_target="tpu_custom_call" | custom-call | tf_op jit(solution)/shard_map/tail_stage/pallas_call | solution.py:509
  43.8 0.8 %copy.21 = bf16[64,4096]{1,0:T(8,128)(2,1)} copy(bf16[64,4096]{1,0:T(8,128)(2,1)S(1)} %tail_stage.1) | data formatting | bytes 1048576
